TPU v7x, 32 devices: a whole 2x2x4 slice. The times are simulated.
32 devices in a mesh: frag: 4 (over x, y), dev: 8 (over z, core).
Axes of the slice: x: 2, y: 2, z: 4, core: 2. Of those that a mesh axis runs over, the one named last changes fastest.
Arguments:
- ao_ints: bfloat16 [256, 64, 64, 64], P(('frag', 'dev')), parts along dimension 0
- coeffs: bfloat16 [256, 64], P('frag'), parts along dimension 0
Outputs:
- output: float32 [256, 64, 4096], P('frag', None, 'dev'), parts along dimension 0
There are 4 independent parts. A program takes and returns all parts, laid end to end along the dimension named above; each array names one.
All inputs are finite; a program needn't handle non-finite values.
Results may differ from a plain program's by a relative error of at most 0.001.
Values are sent between devices in bfloat16 or wider.
A program may use at most 1 GiB of HBM per device.

v0:
```python
import jax
import jax.numpy as jnp
from jax import lax
from jax.sharding import PartitionSpec as P


def solution(mesh):
    def local_transform(ao_rows, coeffs):
        local_rows = ao_rows.shape[0]
        n_basis = coeffs.shape[0]
        t_one = jnp.einsum('pqrs,rj->pqsj', ao_rows, coeffs, preferred_element_type=jnp.float32).astype(jnp.bfloat16)
        half_ints = jnp.einsum('pqsj,sb->pqjb', t_one, coeffs, preferred_element_type=jnp.float32).astype(jnp.bfloat16)
        h_flat = half_ints.reshape(local_rows, n_basis, n_basis * n_basis)
        full_pq = lax.all_to_all(h_flat, 'dev', split_axis=2, concat_axis=0, tiled=True)
        g_local = jnp.einsum('qa,pqk->apk', coeffs, full_pq, preferred_element_type=jnp.float32).astype(jnp.bfloat16)
        return jnp.einsum('pi,apk->iak', coeffs, g_local, preferred_element_type=jnp.float32)

    return jax.shard_map(local_transform, mesh=mesh, in_specs=(P(('frag', 'dev')), P('frag')), out_specs=P('frag', None, 'dev'), check_vma=False)
```

profile of v0, /device:TPU:1, one launch (start us, length us, event | category | flops | bytes accessed | tf_op | source)
XLA Modules:
  0.0 166.4 jit_solution(8661708740484132071)
XLA Ops:
  0.0 0.0 copy-start
  0.0 0.7 copy-done
  0.7 9.3 %fusion.2 = bf16[8,64,64,64]{3,2,1,0:T(8,128)(2,1)} fusion(bf16[8,64,64,64]{3,2,1,0:T(8,128)(2,1)} %param.2, bf16[64,64]{1,0:T(8,128)(2,1)S(1)} %copy-done), kind=kOutput, calls=%fused_computation.2 | convolution fusion | flops 541065216 | bytes 8396800 | tf_op jit(solution)/shard_map/pqsj,sb->pqjb/dot_general | solution.py:12
  10.0 11.7 %copy.28 = bf16[8,64,64,64]{1,0,3,2:T(8,128)(2,1)} copy(bf16[8,64,64,64]{3,2,1,0:T(8,128)(2,1)} %fusion.2) | data formatting | bytes 8388608 | tf_op jit(solution)/shard_map/reshape | solution.py:13
  21.7 10.5 %reshape.7 = bf16[8,2,131072]{2,1,0:T(2,128)(2,1)} reshape(bf16[4096,8,64]{2,1,0:T(8,128)(2,1)} %bitcast.27) | data formatting | bytes 8388608
  32.2 99.1 %all_to_all.18 = bf16[8,2,131072]{2,1,0:T(2,128)(2,1)} all-to-all(bf16[8,2,131072]{2,1,0:T(2,128)(2,1)} %reshape.7), channel_id=1, replica_groups=mesh['frag'=4,'dev'=8] {'dev'}, dimensions={0} | all-to-all | bytes 8388608 | tf_op jit(solution)/shard_map/all_to_all | solution.py:14
  131.2 10.3 %reshape.8 = bf16[4096,8,64]{2,1,0:T(8,128)(2,1)} reshape(bf16[8,2,131072]{2,1,0:T(2,128)(2,1)} %all_to_all.18) | data formatting | bytes 8388608
  141.5 9.8 %copy.18 = bf16[8,8,64,512]{3,2,1,0:T(8,128)(2,1)} copy(bf16[8,8,64,512]{2,1,3,0:T(8,128)(2,1)} %bitcast.26) | data formatting | bytes 8388608 | tf_op jit(solution)/shard_map/all_to_all | solution.py:14
  151.3 3.5 %convert_bitcast_fusion = bf16[64,64,512]{2,0,1:T(8,128)(2,1)S(1)} fusion(bf16[64,64,512]{2,1,0:T(8,128)(2,1)} %bitcast.28, bf16[64,64]{1,0:T(8,128)(2,1)S(1)} %copy-done), kind=kOutput, calls=%fused_computation.6 | convolution fusion | flops 270532608 | bytes 8396800 | tf_op jit(solution)/shard_map/qa,pqk->apk/dot_general | solution.py:15
  154.8 3.4 %fusion.9 = f32[64,64,512]{2,0,1:T(8,128)S(1)} fusion(bf16[64,64,512]{2,0,1:T(8,128)(2,1)S(1)} %convert_bitcast_fusion, bf16[64,64]{1,0:T(8,128)(2,1)S(1)} %copy-done), kind=kOutput, calls=%fused_computation.7 | convolution fusion | flops 268435456 | bytes 12591104 | tf_op jit(solution)/shard_map/pi,apk->iak/dot_general | solution.py:16
  158.1 8.3 %copy.22 = f32[64,64,512]{2,1,0:T(8,128)} copy(f32[64,64,512]{2,0,1:T(8,128)S(1)} %fusion.9) | data formatting | bytes 16777216 | tf_op jit(solution)/shard_map/pi,apk->iak/dot_general | solution.py:16
Async XLA Ops:
  0.0 0.7 copy-start
where the time goes:
time: 169 us; the launch traced here: 166 us
  blocking collectives  99.1 us (59%)
  local copies, waits for them, and re-layouts  51.2 us (30%)
  matrix products  16.1 us (10%)
    all_to_all x1, blocking collectives, local_transform(): lax.all_to_all(h_flat, 'dev', split_axis=2, concat_axis=0, tiled=True)  99.1 us
    unnamed x4, local copies, waits for them, and re-layouts  21.5 us
    reshape x1, local copies, waits for them, and re-layouts, local_transform(): h_flat = half_ints.reshape(local_rows, n_basis, n_basis * n_basis)  11.7 us
    all_to_all x1, local copies, waits for them, and re-layouts, local_transform(): lax.all_to_all(h_flat, 'dev', split_axis=2, concat_axis=0, tiled=True)  9.76 us
    dot_general x1, matrix products, local_transform(): jnp.einsum('pqsj,sb->pqjb', t_one, coeffs, preferred_element_type=jnp.flo...  9.28 us
    dot_general x1, local copies, waits for them, and re-layouts, local_transform(): jnp.einsum('pi,apk->iak', coeffs, g_local, preferred_element_type=jnp.flo...  8.26 us
    dot_general x1, matrix products, local_transform(): jnp.einsum('qa,pqk->apk', coeffs, full_pq, preferred_element_type=jnp.flo...  3.48 us

commit v1 on v0

v1 whole, which is shorter than its diff:
```python
import functools

import jax
import jax.numpy as jnp
from jax import lax
from jax.experimental import pallas as pl
from jax.experimental.pallas import tpu as pltpu
from jax.sharding import PartitionSpec as P

N = 64
DEV = 8
ROWS = N // DEV
COLS = N * N // DEV
BF16 = jnp.bfloat16
F32 = jnp.float32


def iota(shape, dim):
    return lax.broadcasted_iota(jnp.int32, shape, dim)


def exchange_kernel(a_hbm, c_hbm, g_ref, l4_ref, a_vm, c_vm, l_vm, b4_vm, ct_vm, send, recv, a_sem, c_sem, send_sem, recv_sem):
    me = lax.axis_index("dev")
    chip = me // 2
    core = me % 2

    load_c = pltpu.make_async_copy(c_hbm, c_vm, c_sem)
    load_c.start()

    def load_row(p):
        return pltpu.make_async_copy(a_hbm.at[p], a_vm.at[p], a_sem.at[p])

    for p in range(ROWS):
        load_row(p).start()

    barrier = pltpu.get_barrier_semaphore()
    for k in range(1, DEV):
        pl.semaphore_signal(barrier, inc=1, device_id={"dev": (me + k) % DEV}, device_id_type=pl.DeviceIdType.MESH)

    load_c.wait()
    c = c_vm[...]
    spread = (iota((8 * N, N), 0) // 8 == iota((8 * N, N), 1)).astype(BF16)
    nt = (((1,), (1,)), ((), ()))
    rows = lax.dot_general(spread, c, nt, preferred_element_type=F32)
    wide = (8 * N, 8 * N)
    pair = jnp.concatenate([rows, rows], axis=1)
    tiled = jnp.concatenate([pair] * 4, axis=1)
    l_vm[...] = jnp.where(iota(wide, 0) % 8 == iota(wide, 1) // N, tiled, 0.0).astype(BF16)
    widen = (iota((N, 8 * N), 0) == iota((N, 8 * N), 1) // 8).astype(BF16)
    full = jnp.dot(rows.astype(BF16), widen, preferred_element_type=F32)
    l4_ref[...] = jnp.where(iota(wide, 0) % 8 == iota(wide, 1) % 8, full, 0.0).astype(BF16)
    cf = c.astype(F32)
    cpair = jnp.concatenate([cf, cf], axis=1)
    c4 = jnp.concatenate([cpair, cpair], axis=1)
    c44 = jnp.concatenate([c4] * 4, axis=0)
    quad = (4 * N, 4 * N)
    b4_vm[...] = jnp.where(iota(quad, 0) // N == iota(quad, 1) // N, c44, 0.0).astype(BF16)
    eye = (iota((N, N), 0) == iota((N, N), 1)).astype(BF16)
    ct_vm[...] = lax.dot_general(eye, c, nt, preferred_element_type=F32).astype(BF16)

    pl.semaphore_wait(barrier, DEV - 1)

    def block(p, dest):
        return pltpu.make_async_remote_copy(
            src_ref=send.at[dest, p],
            dst_ref=recv.at[me, p],
            send_sem=send_sem.at[dest, p],
            recv_sem=recv_sem.at[me, p],
            device_id={"dev": dest},
            device_id_type=pl.DeviceIdType.MESH,
        )

    low = iota((32, 8, 128), 2) < N

    def half_row(p, h):
        a = a_vm[p, pl.ds(32 * h, 32)].reshape(4, 8 * N, N)
        left = jnp.concatenate([a[0], a[1]], axis=1)
        right = jnp.concatenate([a[2], a[3]], axis=1)
        a4 = jnp.concatenate([left, right], axis=1)
        t_one = jnp.dot(l_vm[...], a4, preferred_element_type=F32).astype(BF16)
        half = jnp.dot(t_one, b4_vm[...], preferred_element_type=F32)
        pairs = half.reshape(32, 2, 8, 256)
        for t in range(2):
            even = pairs[:, 0, :, 128 * t:128 * t + 128]
            odd = pairs[:, 1, :, 128 * t:128 * t + 128]
            first = jnp.where(low, even, pltpu.roll(odd, N, 2))
            second = jnp.where(low, pltpu.roll(even, N, 2), odd)
            both = jnp.concatenate([first, second], axis=1).astype(BF16)
            for jp in range(32):
                send[jp // 4, p, pl.ds(32 * h + 16 * t, 16), pl.ds(128 * (jp % 4), 128)] = both[jp]

    is_edge = jnp.logical_or(chip == 0, chip == 3)
    inward = jnp.where(chip < 2, 1, -1)
    edge_near = chip + inward
    mid_cross, mid_far, mid_back = chip + inward, chip + 2 * inward, chip - inward

    def send_row(p):
        block(p, 2 * chip + 1 - core).start()

        @pl.when(is_edge)
        def _():
            for k in range(2):
                block(p, 2 * edge_near + k).start()

        @pl.when(jnp.logical_not(is_edge))
        def _():
            for other in (mid_cross, mid_far, mid_back):
                for k in range(2):
                    block(p, 2 * other + k).start()

    def make_row(p, carry):
        load_row(p).wait()
        for h in range(2):
            half_row(p, h)
        send_row(p)
        return carry

    lax.fori_loop(0, ROWS, make_row, 0)

    @pl.when(is_edge)
    def _():
        def far_row(p, carry):
            for step in (2, 3):
                for k in range(2):
                    block(p, 2 * (chip + step * inward) + k).start()
            return carry

        lax.fori_loop(0, ROWS, far_row, 0)

    def third(src, p, first, second):
        g0 = jnp.dot(ct_vm[...], first, preferred_element_type=F32).reshape(8, 8, COLS)
        g1 = jnp.dot(ct_vm[...], second, preferred_element_type=F32).reshape(8, 8, COLS)
        at = pl.multiple_of(N * src + 8 * p, 16)
        g_ref[:, pl.ds(at, 16), :] = jnp.concatenate([g0, g1], axis=1).astype(BF16)

    def own(t, carry):
        third(me, 2 * t, send[me, 2 * t], send[me, 2 * t + 1])
        return carry

    lax.fori_loop(0, ROWS // 2, own, 0)

    def arrived(src, p):
        pltpu.make_async_remote_copy(
            src_ref=send.at[src, p],
            dst_ref=recv.at[src, p],
            send_sem=send_sem.at[src, p],
            recv_sem=recv_sem.at[src, p],
            device_id={"dev": src},
            device_id_type=pl.DeviceIdType.MESH,
        ).wait_recv()

    def take(src):
        def body(t, carry):
            arrived(src, 2 * t)
            arrived(src, 2 * t + 1)
            third(src, 2 * t, recv[src, 2 * t], recv[src, 2 * t + 1])
            return carry

        lax.fori_loop(0, ROWS // 2, body, 0)

    take(2 * chip + 1 - core)
    order = [
        jnp.where(is_edge, chip + inward, chip - inward),
        jnp.where(is_edge, chip + 2 * inward, chip + inward),
        jnp.where(is_edge, chip + 3 * inward, chip + 2 * inward),
    ]
    for other in order:
        for k in range(2):
            take(2 * other + k)

    def sent(p, carry):
        for k in range(1, DEV):
            block(p, (me + k) % DEV).wait_send()
        return carry

    lax.fori_loop(0, ROWS, sent, 0)


def fourth_kernel(g_ref, l4_ref, v_hbm, v_vm, v_sem):
    def put(ag):
        return pltpu.make_async_copy(v_vm.at[ag], v_hbm.at[:, pl.ds(8 * ag, 8), :], v_sem.at[ag])

    for ag in range(8):
        v_vm[ag] = jnp.dot(l4_ref[...], g_ref[ag], preferred_element_type=F32).reshape(N, 8, COLS)
        put(ag).start()
    for ag in range(8):
        put(ag).wait()


def solution(mesh):
    def local_transform(ao_rows, coeffs):
        vmem = pl.BlockSpec(memory_space=pltpu.VMEM)
        anywhere = pl.BlockSpec(memory_space=pltpu.HBM)
        g, l4 = pl.pallas_call(
            exchange_kernel,
            out_shape=(
                jax.ShapeDtypeStruct((8, 8 * N, COLS), BF16),
                jax.ShapeDtypeStruct((8 * N, 8 * N), BF16),
            ),
            in_specs=[anywhere, anywhere],
            out_specs=(vmem, vmem),
            scratch_shapes=[
                pltpu.VMEM((ROWS, N, N, N), BF16),
                pltpu.VMEM((N, N), BF16),
                pltpu.VMEM((8 * N, 8 * N), BF16),
                pltpu.VMEM((4 * N, 4 * N), BF16),
                pltpu.VMEM((N, N), BF16),
                pltpu.VMEM((DEV, ROWS, N, COLS), BF16),
                pltpu.VMEM((DEV, ROWS, N, COLS), BF16),
                pltpu.SemaphoreType.DMA((ROWS,)),
                pltpu.SemaphoreType.DMA,
                pltpu.SemaphoreType.DMA((DEV, ROWS)),
                pltpu.SemaphoreType.DMA((DEV, ROWS)),
            ],
            compiler_params=pltpu.CompilerParams(collective_id=0, has_side_effects=True, vmem_limit_bytes=56 * 2**20),
            name="exchange",
        )(ao_rows, coeffs)
        return pl.pallas_call(
            fourth_kernel,
            out_shape=jax.ShapeDtypeStruct((N, N, COLS), F32),
            in_specs=[vmem, vmem],
            out_specs=anywhere,
            scratch_shapes=[pltpu.VMEM((8, N, 8, COLS), F32), pltpu.SemaphoreType.DMA((8,))],
            compiler_params=pltpu.CompilerParams(vmem_limit_bytes=24 * 2**20),
            name="fourth",
        )(g, l4)

    return jax.shard_map(local_transform, mesh=mesh, in_specs=(P(('frag', 'dev')), P('frag')), out_specs=P('frag', None, 'dev'), check_vma=False)
```

time: 169 us -> 112 us (0.66); the launches traced: 166 us -> 112 us
  Pallas kernels: 0 us -> 108 us
  blocking collectives: 99.1 us -> 0 us
  local copies, waits for them, and re-layouts: 51.2 us -> 3.22 us
  matrix products: 16.1 us -> 0 us
    pallas_call x0 -> x2, Pallas kernels: none -> 108 us  [the longest x1 105 us: local_transform(): pl.pallas_call(exchange_kernel, out_shape=(jax.ShapeDtypeStruct((8, 8 * N...]
    all_to_all x1 -> x0, blocking collectives: 99.1 us -> none  [local_transform(): lax.all_to_all(h_flat, 'dev', split_axis=2, concat_axis=0, tiled=True)]
    unnamed x4, local copies, waits for them, and re-layouts: 21.5 us -> 3.22 us
    dot_general x3 -> x0, matrix products: 16.1 us -> none  [the longest x1 9.28 us: local_transform(): jnp.einsum('pqsj,sb->pqjb', t_one, coeffs, preferred_element_type=jnp.flo...]
    reshape x1 -> x0, local copies, waits for them, and re-layouts: 11.7 us -> none  [local_transform(): h_flat = half_ints.reshape(local_rows, n_basis, n_basis * n_basis)]
    all_to_all x1 -> x0, local copies, waits for them, and re-layouts: 9.76 us -> none  [local_transform(): lax.all_to_all(h_flat, 'dev', split_axis=2, concat_axis=0, tiled=True)]
    dot_general x1 -> x0, local copies, waits for them, and re-layouts: 8.26 us -> none  [local_transform(): jnp.einsum('pi,apk->iak', coeffs, g_local, preferred_element_type=jnp.flo...]
where the time goes in v1:
time: 112 us
  Pallas kernels  108 us (96%)
  local copies, waits for them, and re-layouts  3.22 us (3%)
    pallas_call x1, Pallas kernels, local_transform(): pl.pallas_call(exchange_kernel, out_shape=(jax.ShapeDtypeStruct((8, 8 * N...  105 us
    pallas_call x1, Pallas kernels, local_transform(): pl.pallas_call(fourth_kernel, out_shape=jax.ShapeDtypeStruct((N, N, COLS)...  3.8 us
    unnamed x4, local copies, waits for them, and re-layouts  3.22 us

profile of v1, /device:TPU:1, one launch (start us, length us, event | category | flops | bytes accessed | tf_op | source)
XLA Modules:
  0.0 111.7 jit_solution(14377025483412406981)
XLA Ops:
  0.0 104.6 %exchange.1 = (bf16[8,512,512]{2,1,0:T(8,128)(2,1)}, bf16[512,512]{1,0:T(8,128)(2,1)}) custom-call(bf16[8,64,64,64]{3,2,1,0:T(8,128)(2,1)} %a_hbm.1, bf16[64,64]{1,0:T(8,128)(2,1)} %c_hbm.1), custom_call_target="tpu_custom_call" | custom-call | tf_op jit(solution)/shard_map/exchange/pallas_call | solution.py:194
  104.6 0.0 copy-start
  104.6 2.2 %copy-done = bf16[8,512,512]{2,1,0:T(8,128)(2,1)S(1)} copy-done((bf16[8,512,512]{2,1,0:T(8,128)(2,1)S(1)}, bf16[8,512,512]{2,1,0:T(8,128)(2,1)}, u32[]{:S(2)}) %copy-start) | copy-done | bytes 4194328
  106.8 0.0 copy-start.1
  106.8 1.0 copy-done.1
  107.8 3.8 %fourth.1 = f32[64,64,512]{2,1,0:T(8,128)} custom-call(bf16[8,512,512]{2,1,0:T(8,128)(2,1)S(1)} %copy-done, bf16[512,512]{1,0:T(8,128)(2,1)S(1)} %copy-done.1), custom_call_target="tpu_custom_call" | custom-call | tf_op jit(solution)/shard_map/fourth/pallas_call | solution.py:218
Async XLA Ops:
  104.6 2.2 %copy-start = (bf16[8,512,512]{2,1,0:T(8,128)(2,1)S(1)}, bf16[8,512,512]{2,1,0:T(8,128)(2,1)}, u32[]{:S(2)}) copy-start(bf16[8,512,512]{2,1,0:T(8,128)(2,1)} %get-tuple-element.7.g_ref) | copy-start | bytes 12582916
  106.8 1.0 copy-start.1

commit v2 on v1

--- a/solution.py
+++ b/solution.py
@@ -117,15 +117,21 @@
 
     lax.fori_loop(0, ROWS, make_row, 0)
 
+    def far_rows(dest):
+        return pltpu.make_async_remote_copy(
+            src_ref=send.at[dest],
+            dst_ref=recv.at[me],
+            send_sem=send_sem.at[dest, 0],
+            recv_sem=recv_sem.at[me, 0],
+            device_id={"dev": dest},
+            device_id_type=pl.DeviceIdType.MESH,
+        )
+
     @pl.when(is_edge)
     def _():
-        def far_row(p, carry):
-            for step in (2, 3):
-                for k in range(2):
-                    block(p, 2 * (chip + step * inward) + k).start()
-            return carry
-
-        lax.fori_loop(0, ROWS, far_row, 0)
+        for step in (2, 3):
+            for k in range(2):
+                far_rows(2 * (chip + step * inward) + k).start()
 
     def third(src, p, first, second):
         g0 = jnp.dot(ct_vm[...], first, preferred_element_type=F32).reshape(8, 8, COLS)
@@ -164,16 +170,52 @@
         jnp.where(is_edge, chip + 2 * inward, chip + inward),
         jnp.where(is_edge, chip + 3 * inward, chip + 2 * inward),
     ]
-    for other in order:
+    for other in order[:2]:
         for k in range(2):
             take(2 * other + k)
 
-    def sent(p, carry):
-        for k in range(1, DEV):
-            block(p, (me + k) % DEV).wait_send()
+    def take_far(src):
+        pltpu.make_async_remote_copy(
+            src_ref=send.at[src],
+            dst_ref=recv.at[src],
+            send_sem=send_sem.at[src, 0],
+            recv_sem=recv_sem.at[src, 0],
+            device_id={"dev": src},
+            device_id_type=pl.DeviceIdType.MESH,
+        ).wait_recv()
+
+        def body(t, carry):
+            third(src, 2 * t, recv[src, 2 * t], recv[src, 2 * t + 1])
+            return carry
+
+        lax.fori_loop(0, ROWS // 2, body, 0)
+
+    for k in range(2):
+        take_far(2 * order[2] + k)
+
+    def sent_row(p, carry):
+        block(p, 2 * chip + 1 - core).wait_send()
+
+        @pl.when(is_edge)
+        def _():
+            for k in range(2):
+                block(p, 2 * edge_near + k).wait_send()
+
+        @pl.when(jnp.logical_not(is_edge))
+        def _():
+            for other in (mid_cross, mid_far, mid_back):
+                for k in range(2):
+                    block(p, 2 * other + k).wait_send()
+
         return carry
 
-    lax.fori_loop(0, ROWS, sent, 0)
+    lax.fori_loop(0, ROWS, sent_row, 0)
+
+    @pl.when(is_edge)
+    def _():
+        for step in (2, 3):
+            for k in range(2):
+                far_rows(2 * (chip + step * inward) + k).wait_send()
 
 
 def fourth_kernel(g_ref, l4_ref, v_hbm, v_vm, v_sem):
@@ -212,7 +254,7 @@
                 pltpu.SemaphoreType.DMA((DEV, ROWS)),
                 pltpu.SemaphoreType.DMA((DEV, ROWS)),
             ],
-            compiler_params=pltpu.CompilerParams(collective_id=0, has_side_effects=True, vmem_limit_bytes=56 * 2**20),
+            compiler_params=pltpu.CompilerParams(collective_id=0, has_side_effects=True, vmem_limit_bytes=53 * 2**20),
             name="exchange",
         )(ao_rows, coeffs)
         return pl.pallas_call(

time: 112 us -> 110 us (0.982)
    pallas_call x1, Pallas kernels: 105 us -> 103 us  [local_transform(): pl.pallas_call(exchange_kernel, out_shape=(jax.ShapeDtypeStruct((8, 8 * N...]
where the time goes in v2:
time: 110 us
  Pallas kernels  107 us (97%)
  local copies, waits for them, and re-layouts  2.9 us (3%)
    pallas_call x1, Pallas kernels, local_transform(): pl.pallas_call(exchange_kernel, out_shape=(jax.ShapeDtypeStruct((8, 8 * N...  103 us
    pallas_call x1, Pallas kernels, local_transform(): pl.pallas_call(fourth_kernel, out_shape=jax.ShapeDtypeStruct((N, N, COLS)...  3.8 us
    unnamed x4, local copies, waits for them, and re-layouts  2.9 us

profile of v2, /device:TPU:1, one launch (start us, length us, event | category | flops | bytes accessed | tf_op | source)
XLA Modules:
  0.0 109.5 jit_solution(556233767989561748)
XLA Ops:
  0.0 0.0 copy-start.1
  0.0 0.7 copy-done.1
  0.7 102.8 %exchange.1 = (bf16[8,512,512]{2,1,0:T(8,128)(2,1)}, bf16[512,512]{1,0:T(8,128)(2,1)S(1)}) custom-call(bf16[8,64,64,64]{3,2,1,0:T(8,128)(2,1)} %a_hbm.1, bf16[64,64]{1,0:T(8,128)(2,1)S(1)} %copy-done.1), custom_call_target="tpu_custom_call" | custom-call | tf_op jit(solution)/shard_map/exchange/pallas_call | solution.py:236
  103.5 0.0 copy-start
  103.5 2.2 %copy-done = bf16[8,512,512]{2,1,0:T(8,128)(2,1)S(1)} copy-done((bf16[8,512,512]{2,1,0:T(8,128)(2,1)S(1)}, bf16[8,512,512]{2,1,0:T(8,128)(2,1)}, u32[]{:S(2)}) %copy-start) | copy-done | bytes 4194328
  105.7 3.8 %fourth.1 = f32[64,64,512]{2,1,0:T(8,128)} custom-call(bf16[8,512,512]{2,1,0:T(8,128)(2,1)S(1)} %copy-done, bf16[512,512]{1,0:T(8,128)(2,1)S(1)} %get-tuple-element.8.l4_ref), custom_call_target="tpu_custom_call" | custom-call | tf_op jit(solution)/shard_map/fourth/pallas_call | solution.py:260
Async XLA Ops:
  0.0 0.7 copy-start.1
  103.5 2.2 %copy-start = (bf16[8,512,512]{2,1,0:T(8,128)(2,1)S(1)}, bf16[8,512,512]{2,1,0:T(8,128)(2,1)}, u32[]{:S(2)}) copy-start(bf16[8,512,512]{2,1,0:T(8,128)(2,1)} %get-tuple-element.7.g_ref) | copy-start | bytes 12582916

commit v3 on v2

--- a/solution.py
+++ b/solution.py
@@ -254,9 +254,9 @@
                 pltpu.SemaphoreType.DMA((DEV, ROWS)),
                 pltpu.SemaphoreType.DMA((DEV, ROWS)),
             ],
-            compiler_params=pltpu.CompilerParams(collective_id=0, has_side_effects=True, vmem_limit_bytes=53 * 2**20),
+            compiler_params=pltpu.CompilerParams(collective_id=0, has_side_effects=True, vmem_limit_bytes=48 * 2**20),
             name="exchange",
-        )(ao_rows, coeffs)
+        )(pltpu.with_memory_space_constraint(ao_rows, pltpu.HBM), pltpu.with_memory_space_constraint(coeffs, pltpu.HBM))
         return pl.pallas_call(
             fourth_kernel,
             out_shape=jax.ShapeDtypeStruct((N, N, COLS), F32),

time: 110 us -> 106 us (0.964)
  local copies, waits for them, and re-layouts: 2.9 us -> 0 us
    unnamed x4 -> x0, local copies, waits for them, and re-layouts: 2.9 us -> none
where the time goes in v3:
time: 106 us
  Pallas kernels  106 us (100%)
    pallas_call x1, Pallas kernels, local_transform(): pl.pallas_call(exchange_kernel, out_shape=(jax.ShapeDtypeStruct((8, 8 * N...  102 us
    pallas_call x1, Pallas kernels, local_transform(): pl.pallas_call(fourth_kernel, out_shape=jax.ShapeDtypeStruct((N, N, COLS)...  3.8 us

profile of v3, /device:TPU:1, one launch (start us, length us, event | category | flops | bytes accessed | tf_op | source)
XLA Modules:
  0.0 106.1 jit_solution(7169872575828204379)
XLA Ops:
  0.0 102.3 %exchange.1 = (bf16[8,512,512]{2,1,0:T(8,128)(2,1)S(1)}, bf16[512,512]{1,0:T(8,128)(2,1)S(1)}) custom-call(bf16[8,64,64,64]{3,2,1,0:T(8,128)(2,1)} %a_hbm.1, bf16[64,64]{1,0:T(8,128)(2,1)} %c_hbm.1), custom_call_target="tpu_custom_call" | custom-call | tf_op jit(solution)/shard_map/exchange/pallas_call | solution.py:236
  102.3 3.8 %fourth.1 = f32[64,64,512]{2,1,0:T(8,128)} custom-call(bf16[8,512,512]{2,1,0:T(8,128)(2,1)S(1)} %get-tuple-element.7.g_ref, bf16[512,512]{1,0:T(8,128)(2,1)S(1)} %get-tuple-element.8.l4_ref), custom_call_target="tpu_custom_call" | custom-call | tf_op jit(solution)/shard_map/fourth/pallas_call | solution.py:260

commit v4 on v1

--- a/solution.py
+++ b/solution.py
@@ -91,22 +91,21 @@
 
     is_edge = jnp.logical_or(chip == 0, chip == 3)
     inward = jnp.where(chip < 2, 1, -1)
-    edge_near = chip + inward
-    mid_cross, mid_far, mid_back = chip + inward, chip + 2 * inward, chip - inward
+    partner = 2 * chip + 1 - core
+    near = chip + inward
+    far = chip + 2 * inward
+    last = chip + 3 * inward
+    outward = chip - inward
 
     def send_row(p):
-        block(p, 2 * chip + 1 - core).start()
-
-        @pl.when(is_edge)
+        block(p, partner).start()
+        for k in range(2):
+            block(p, 2 * near + k).start()
+
+        @pl.when(jnp.logical_not(is_edge))
         def _():
             for k in range(2):
-                block(p, 2 * edge_near + k).start()
-
-        @pl.when(jnp.logical_not(is_edge))
-        def _():
-            for other in (mid_cross, mid_far, mid_back):
-                for k in range(2):
-                    block(p, 2 * other + k).start()
+                block(p, 2 * outward + k).start()
 
     def make_row(p, carry):
         load_row(p).wait()
@@ -117,15 +116,15 @@
 
     lax.fori_loop(0, ROWS, make_row, 0)
 
-    @pl.when(is_edge)
-    def _():
-        def far_row(p, carry):
-            for step in (2, 3):
-                for k in range(2):
-                    block(p, 2 * (chip + step * inward) + k).start()
-            return carry
-
-        lax.fori_loop(0, ROWS, far_row, 0)
+    def rows(dest, src):
+        return pltpu.make_async_remote_copy(
+            src_ref=send.at[dest],
+            dst_ref=recv.at[src],
+            send_sem=send_sem.at[dest, 0],
+            recv_sem=recv_sem.at[src, 0],
+            device_id={"dev": dest},
+            device_id_type=pl.DeviceIdType.MESH,
+        )
 
     def third(src, p, first, second):
         g0 = jnp.dot(ct_vm[...], first, preferred_element_type=F32).reshape(8, 8, COLS)
@@ -139,41 +138,82 @@
 
     lax.fori_loop(0, ROWS // 2, own, 0)
 
-    def arrived(src, p):
-        pltpu.make_async_remote_copy(
-            src_ref=send.at[src, p],
-            dst_ref=recv.at[src, p],
-            send_sem=send_sem.at[src, p],
-            recv_sem=recv_sem.at[src, p],
-            device_id={"dev": src},
-            device_id_type=pl.DeviceIdType.MESH,
-        ).wait_recv()
-
-    def take(src):
+    def await_rows(src):
+        def body(p, carry):
+            pltpu.make_async_remote_copy(
+                src_ref=send.at[src, p],
+                dst_ref=recv.at[src, p],
+                send_sem=send_sem.at[src, p],
+                recv_sem=recv_sem.at[src, p],
+                device_id={"dev": src},
+                device_id_type=pl.DeviceIdType.MESH,
+            ).wait_recv()
+            return carry
+
+        lax.fori_loop(0, ROWS, body, 0)
+
+    def third_rows(src):
         def body(t, carry):
-            arrived(src, 2 * t)
-            arrived(src, 2 * t + 1)
             third(src, 2 * t, recv[src, 2 * t], recv[src, 2 * t + 1])
             return carry
 
         lax.fori_loop(0, ROWS // 2, body, 0)
 
-    take(2 * chip + 1 - core)
-    order = [
-        jnp.where(is_edge, chip + inward, chip - inward),
-        jnp.where(is_edge, chip + 2 * inward, chip + inward),
-        jnp.where(is_edge, chip + 3 * inward, chip + 2 * inward),
-    ]
-    for other in order:
-        for k in range(2):
-            take(2 * other + k)
-
-    def sent(p, carry):
-        for k in range(1, DEV):
-            block(p, (me + k) % DEV).wait_send()
-        return carry
-
-    lax.fori_loop(0, ROWS, sent, 0)
+    def sent_rows(dest):
+        def body(p, carry):
+            block(p, dest).wait_send()
+            return carry
+
+        lax.fori_loop(0, ROWS, body, 0)
+
+    await_rows(partner)
+    third_rows(partner)
+
+    for k in range(2):
+        sent_rows(2 * near + k)
+    for k in range(2):
+        rows(2 * far + k, me).start()
+
+    beside = jnp.where(is_edge, near, outward)
+    for k in range(2):
+        await_rows(2 * beside + k)
+        third_rows(2 * beside + k)
+
+    @pl.when(is_edge)
+    def _():
+        for k in range(2):
+            rows(2 * far + k, me).wait_send()
+        for k in range(2):
+            rows(2 * last + k, me).start()
+        for k in range(2):
+            rows(2 * far + k, 2 * far + k).wait_recv()
+
+    @pl.when(jnp.logical_not(is_edge))
+    def _():
+        for k in range(2):
+            await_rows(2 * near + k)
+
+    second = jnp.where(is_edge, far, near)
+    for k in range(2):
+        third_rows(2 * second + k)
+
+    third_chip = jnp.where(is_edge, last, far)
+    for k in range(2):
+        rows(2 * third_chip + k, 2 * third_chip + k).wait_recv()
+        third_rows(2 * third_chip + k)
+
+    sent_rows(partner)
+
+    @pl.when(is_edge)
+    def _():
+        for k in range(2):
+            rows(2 * last + k, me).wait_send()
+
+    @pl.when(jnp.logical_not(is_edge))
+    def _():
+        for k in range(2):
+            rows(2 * far + k, me).wait_send()
+            sent_rows(2 * outward + k)
 
 
 def fourth_kernel(g_ref, l4_ref, v_hbm, v_vm, v_sem):
@@ -212,9 +252,9 @@
                 pltpu.SemaphoreType.DMA((DEV, ROWS)),
                 pltpu.SemaphoreType.DMA((DEV, ROWS)),
             ],
-            compiler_params=pltpu.CompilerParams(collective_id=0, has_side_effects=True, vmem_limit_bytes=56 * 2**20),
+            compiler_params=pltpu.CompilerParams(collective_id=0, has_side_effects=True, vmem_limit_bytes=48 * 2**20),
             name="exchange",
-        )(ao_rows, coeffs)
+        )(pltpu.with_memory_space_constraint(ao_rows, pltpu.HBM), pltpu.with_memory_space_constraint(coeffs, pltpu.HBM))
         return pl.pallas_call(
             fourth_kernel,
             out_shape=jax.ShapeDtypeStruct((N, N, COLS), F32),

time: 112 us -> 107 us (0.955)
  local copies, waits for them, and re-layouts: 3.22 us -> 0 us
    unnamed x4 -> x0, local copies, waits for them, and re-layouts: 3.22 us -> none
    pallas_call x1, Pallas kernels: 105 us -> 103 us  [local_transform(): pl.pallas_call(exchange_kernel, out_shape=(jax.ShapeDtypeStruct((8, 8 * N...]
where the time goes in v4:
time: 107 us
  Pallas kernels  107 us (100%)
    pallas_call x1, Pallas kernels, local_transform(): pl.pallas_call(exchange_kernel, out_shape=(jax.ShapeDtypeStruct((8, 8 * N...  103 us
    pallas_call x1, Pallas kernels, local_transform(): pl.pallas_call(fourth_kernel, out_shape=jax.ShapeDtypeStruct((N, N, COLS)...  3.8 us

profile of v4, /device:TPU:1, one launch (start us, length us, event | category | flops | bytes accessed | tf_op | source)
XLA Modules:
  0.0 106.9 jit_solution(6724841319392915900)
XLA Ops:
  0.0 103.1 %exchange.1 = (bf16[8,512,512]{2,1,0:T(8,128)(2,1)S(1)}, bf16[512,512]{1,0:T(8,128)(2,1)S(1)}) custom-call(bf16[8,64,64,64]{3,2,1,0:T(8,128)(2,1)} %a_hbm.1, bf16[64,64]{1,0:T(8,128)(2,1)} %c_hbm.1), custom_call_target="tpu_custom_call" | custom-call | tf_op jit(solution)/shard_map/exchange/pallas_call | solution.py:234
  103.1 3.8 %fourth.1 = f32[64,64,512]{2,1,0:T(8,128)} custom-call(bf16[8,512,512]{2,1,0:T(8,128)(2,1)S(1)} %get-tuple-element.7.g_ref, bf16[512,512]{1,0:T(8,128)(2,1)S(1)} %get-tuple-element.8.l4_ref), custom_call_target="tpu_custom_call" | custom-call | tf_op jit(solution)/shard_map/fourth/pallas_call | solution.py:258

commit v5 on v1

--- a/solution.py
+++ b/solution.py
@@ -91,41 +91,31 @@
 
     is_edge = jnp.logical_or(chip == 0, chip == 3)
     inward = jnp.where(chip < 2, 1, -1)
-    edge_near = chip + inward
-    mid_cross, mid_far, mid_back = chip + inward, chip + 2 * inward, chip - inward
-
-    def send_row(p):
-        block(p, 2 * chip + 1 - core).start()
-
-        @pl.when(is_edge)
-        def _():
-            for k in range(2):
-                block(p, 2 * edge_near + k).start()
-
-        @pl.when(jnp.logical_not(is_edge))
-        def _():
-            for other in (mid_cross, mid_far, mid_back):
-                for k in range(2):
-                    block(p, 2 * other + k).start()
+    partner = 2 * chip + 1 - core
+    near = chip + inward
+    far = chip + 2 * inward
+    last = chip + 3 * inward
+    outward = chip - inward
+    third_chip = jnp.where(is_edge, last, outward)
 
     def make_row(p, carry):
         load_row(p).wait()
         for h in range(2):
             half_row(p, h)
-        send_row(p)
+        for other in (third_chip, far):
+            for k in range(2):
+                block(p, 2 * other + k).start()
+        block(p, partner).start()
         return carry
 
     lax.fori_loop(0, ROWS, make_row, 0)
 
-    @pl.when(is_edge)
-    def _():
-        def far_row(p, carry):
-            for step in (2, 3):
-                for k in range(2):
-                    block(p, 2 * (chip + step * inward) + k).start()
-            return carry
-
-        lax.fori_loop(0, ROWS, far_row, 0)
+    def near_row(p, carry):
+        for k in range(2):
+            block(p, 2 * near + k).start()
+        return carry
+
+    lax.fori_loop(0, ROWS, near_row, 0)
 
     def third(src, p, first, second):
         g0 = jnp.dot(ct_vm[...], first, preferred_element_type=F32).reshape(8, 8, COLS)
@@ -149,31 +139,26 @@
             device_id_type=pl.DeviceIdType.MESH,
         ).wait_recv()
 
-    def take(src):
+    def take(sources):
         def body(t, carry):
-            arrived(src, 2 * t)
-            arrived(src, 2 * t + 1)
-            third(src, 2 * t, recv[src, 2 * t], recv[src, 2 * t + 1])
+            for src in sources:
+                arrived(src, 2 * t)
+                arrived(src, 2 * t + 1)
+                third(src, 2 * t, recv[src, 2 * t], recv[src, 2 * t + 1])
             return carry
 
         lax.fori_loop(0, ROWS // 2, body, 0)
 
-    take(2 * chip + 1 - core)
-    order = [
-        jnp.where(is_edge, chip + inward, chip - inward),
-        jnp.where(is_edge, chip + 2 * inward, chip + inward),
-        jnp.where(is_edge, chip + 3 * inward, chip + 2 * inward),
-    ]
-    for other in order:
-        for k in range(2):
-            take(2 * other + k)
-
-    def sent(p, carry):
+    take([partner])
+    for other in (third_chip, far, near):
+        take([2 * other, 2 * other + 1])
+
+    def sent_row(p, carry):
         for k in range(1, DEV):
             block(p, (me + k) % DEV).wait_send()
         return carry
 
-    lax.fori_loop(0, ROWS, sent, 0)
+    lax.fori_loop(0, ROWS, sent_row, 0)
 
 
 def fourth_kernel(g_ref, l4_ref, v_hbm, v_vm, v_sem):
@@ -212,9 +197,9 @@
                 pltpu.SemaphoreType.DMA((DEV, ROWS)),
                 pltpu.SemaphoreType.DMA((DEV, ROWS)),
             ],
-            compiler_params=pltpu.CompilerParams(collective_id=0, has_side_effects=True, vmem_limit_bytes=56 * 2**20),
+            compiler_params=pltpu.CompilerParams(collective_id=0, has_side_effects=True, vmem_limit_bytes=48 * 2**20),
             name="exchange",
-        )(ao_rows, coeffs)
+        )(pltpu.with_memory_space_constraint(ao_rows, pltpu.HBM), pltpu.with_memory_space_constraint(coeffs, pltpu.HBM))
         return pl.pallas_call(
             fourth_kernel,
             out_shape=jax.ShapeDtypeStruct((N, N, COLS), F32),

time: 112 us -> 102 us (0.911)
  the two profiles are of different devices: /device:TPU:1 before, /device:TPU:15 now
where the time goes in v5:
time: 102 us
  Pallas kernels  102 us (100%)
    pallas_call x1, Pallas kernels, local_transform(): pl.pallas_call(exchange_kernel, out_shape=(jax.ShapeDtypeStruct((8, 8 * N...  98.2 us
    pallas_call x1, Pallas kernels, local_transform(): pl.pallas_call(fourth_kernel, out_shape=jax.ShapeDtypeStruct((N, N, COLS)...  3.81 us

profile of v5, /device:TPU:15, one launch (start us, length us, event | category | flops | bytes accessed | tf_op | source)
XLA Modules:
  0.0 102.0 jit_solution(13244050038666384833)
XLA Ops:
  0.0 98.2 %exchange.1 = (bf16[8,512,512]{2,1,0:T(8,128)(2,1)S(1)}, bf16[512,512]{1,0:T(8,128)(2,1)S(1)}) custom-call(bf16[8,64,64,64]{3,2,1,0:T(8,128)(2,1)} %a_hbm.1, bf16[64,64]{1,0:T(8,128)(2,1)} %c_hbm.1), custom_call_target="tpu_custom_call" | custom-call | tf_op jit(solution)/shard_map/exchange/pallas_call | solution.py:179
  98.2 3.8 %fourth.1 = f32[64,64,512]{2,1,0:T(8,128)} custom-call(bf16[8,512,512]{2,1,0:T(8,128)(2,1)S(1)} %get-tuple-element.7.g_ref, bf16[512,512]{1,0:T(8,128)(2,1)S(1)} %get-tuple-element.8.l4_ref), custom_call_target="tpu_custom_call" | custom-call | tf_op jit(solution)/shard_map/fourth/pallas_call | solution.py:203

commit v6 on v5

--- a/solution.py
+++ b/solution.py
@@ -103,16 +103,16 @@
         for h in range(2):
             half_row(p, h)
         for other in (third_chip, far):
-            for k in range(2):
-                block(p, 2 * other + k).start()
+            for mine in (core, 1 - core):
+                block(p, 2 * other + mine).start()
         block(p, partner).start()
         return carry
 
     lax.fori_loop(0, ROWS, make_row, 0)
 
     def near_row(p, carry):
-        for k in range(2):
-            block(p, 2 * near + k).start()
+        for mine in (core, 1 - core):
+            block(p, 2 * near + mine).start()
         return carry
 
     lax.fori_loop(0, ROWS, near_row, 0)

time: 102 us -> 102 us (level)
  no operation moved by 1% of the time
where the time goes in v6:
time: 102 us
  Pallas kernels  102 us (100%)
    pallas_call x1, Pallas kernels, local_transform(): pl.pallas_call(exchange_kernel, out_shape=(jax.ShapeDtypeStruct((8, 8 * N...  98.2 us
    pallas_call x1, Pallas kernels, local_transform(): pl.pallas_call(fourth_kernel, out_shape=jax.ShapeDtypeStruct((N, N, COLS)...  3.81 us

profile of v6, /device:TPU:15, one launch (start us, length us, event | category | flops | bytes accessed | tf_op | source)
XLA Modules:
  0.0 102.0 jit_solution(2519459251425130934)
XLA Ops:
  0.0 98.2 %exchange.1 = (bf16[8,512,512]{2,1,0:T(8,128)(2,1)S(1)}, bf16[512,512]{1,0:T(8,128)(2,1)S(1)}) custom-call(bf16[8,64,64,64]{3,2,1,0:T(8,128)(2,1)} %a_hbm.1, bf16[64,64]{1,0:T(8,128)(2,1)} %c_hbm.1), custom_call_target="tpu_custom_call" | custom-call | tf_op jit(solution)/shard_map/exchange/pallas_call | solution.py:179
  98.2 3.8 %fourth.1 = f32[64,64,512]{2,1,0:T(8,128)} custom-call(bf16[8,512,512]{2,1,0:T(8,128)(2,1)S(1)} %get-tuple-element.7.g_ref, bf16[512,512]{1,0:T(8,128)(2,1)S(1)} %get-tuple-element.8.l4_ref), custom_call_target="tpu_custom_call" | custom-call | tf_op jit(solution)/shard_map/fourth/pallas_call | solution.py:203

commit v7 on v6

--- a/solution.py
+++ b/solution.py
@@ -30,8 +30,7 @@
     def load_row(p):
         return pltpu.make_async_copy(a_hbm.at[p], a_vm.at[p], a_sem.at[p])
 
-    for p in range(ROWS):
-        load_row(p).start()
+    load_row(0).start()
 
     barrier = pltpu.get_barrier_semaphore()
     for k in range(1, DEV):
@@ -46,17 +45,12 @@
     pair = jnp.concatenate([rows, rows], axis=1)
     tiled = jnp.concatenate([pair] * 4, axis=1)
     l_vm[...] = jnp.where(iota(wide, 0) % 8 == iota(wide, 1) // N, tiled, 0.0).astype(BF16)
-    widen = (iota((N, 8 * N), 0) == iota((N, 8 * N), 1) // 8).astype(BF16)
-    full = jnp.dot(rows.astype(BF16), widen, preferred_element_type=F32)
-    l4_ref[...] = jnp.where(iota(wide, 0) % 8 == iota(wide, 1) % 8, full, 0.0).astype(BF16)
     cf = c.astype(F32)
     cpair = jnp.concatenate([cf, cf], axis=1)
     c4 = jnp.concatenate([cpair, cpair], axis=1)
     c44 = jnp.concatenate([c4] * 4, axis=0)
     quad = (4 * N, 4 * N)
     b4_vm[...] = jnp.where(iota(quad, 0) // N == iota(quad, 1) // N, c44, 0.0).astype(BF16)
-    eye = (iota((N, N), 0) == iota((N, N), 1)).astype(BF16)
-    ct_vm[...] = lax.dot_general(eye, c, nt, preferred_element_type=F32).astype(BF16)
 
     pl.semaphore_wait(barrier, DEV - 1)
 
@@ -100,6 +94,12 @@
 
     def make_row(p, carry):
         load_row(p).wait()
+
+        @pl.when(p == 0)
+        def _():
+            for later in range(1, ROWS):
+                load_row(later).start()
+
         for h in range(2):
             half_row(p, h)
         for other in (third_chip, far):
@@ -116,6 +116,14 @@
         return carry
 
     lax.fori_loop(0, ROWS, near_row, 0)
+
+    c = c_vm[...]
+    rows = lax.dot_general(spread, c, nt, preferred_element_type=F32)
+    widen = (iota((N, 8 * N), 0) == iota((N, 8 * N), 1) // 8).astype(BF16)
+    full = jnp.dot(rows.astype(BF16), widen, preferred_element_type=F32)
+    l4_ref[...] = jnp.where(iota(wide, 0) % 8 == iota(wide, 1) % 8, full, 0.0).astype(BF16)
+    eye = (iota((N, N), 0) == iota((N, N), 1)).astype(BF16)
+    ct_vm[...] = lax.dot_general(eye, c, nt, preferred_element_type=F32).astype(BF16)
 
     def third(src, p, first, second):
         g0 = jnp.dot(ct_vm[...], first, preferred_element_type=F32).reshape(8, 8, COLS)

time: 102 us -> 101 us (level)
  Pallas kernels: 102 us -> 100 us
    pallas_call x1, Pallas kernels: 98.2 us -> 96.7 us  [local_transform(): pl.pallas_call(exchange_kernel, out_shape=(jax.ShapeDtypeStruct((8, 8 * N...]
where the time goes in v7:
time: 101 us; the launch traced here: 100 us
  Pallas kernels  100 us (99%)
    pallas_call x1, Pallas kernels, local_transform(): pl.pallas_call(exchange_kernel, out_shape=(jax.ShapeDtypeStruct((8, 8 * N...  96.7 us
    pallas_call x1, Pallas kernels, local_transform(): pl.pallas_call(fourth_kernel, out_shape=jax.ShapeDtypeStruct((N, N, COLS)...  3.8 us

profile of v7, /device:TPU:15, one launch (start us, length us, event | category | flops | bytes accessed | tf_op | source)
XLA Modules:
  0.0 100.5 jit_solution(15743721250241878571)
XLA Ops:
  0.0 96.7 %exchange.1 = (bf16[8,512,512]{2,1,0:T(8,128)(2,1)S(1)}, bf16[512,512]{1,0:T(8,128)(2,1)S(1)}) custom-call(bf16[8,64,64,64]{3,2,1,0:T(8,128)(2,1)} %a_hbm.1, bf16[64,64]{1,0:T(8,128)(2,1)} %c_hbm.1), custom_call_target="tpu_custom_call" | custom-call | tf_op jit(solution)/shard_map/exchange/pallas_call | solution.py:187
  96.7 3.8 %fourth.1 = f32[64,64,512]{2,1,0:T(8,128)} custom-call(bf16[8,512,512]{2,1,0:T(8,128)(2,1)S(1)} %get-tuple-element.7.g_ref, bf16[512,512]{1,0:T(8,128)(2,1)S(1)} %get-tuple-element.8.l4_ref), custom_call_target="tpu_custom_call" | custom-call | tf_op jit(solution)/shard_map/fourth/pallas_call | solution.py:211

commit v8 on v7

--- a/solution.py
+++ b/solution.py
@@ -11,6 +11,7 @@
 DEV = 8
 ROWS = N // DEV
 COLS = N * N // DEV
+NEAR_GROUPS = ((0, 4), (4, 2), (6, 2))
 BF16 = jnp.bfloat16
 F32 = jnp.float32
 
@@ -110,12 +111,31 @@
 
     lax.fori_loop(0, ROWS, make_row, 0)
 
-    def near_row(p, carry):
-        for mine in (core, 1 - core):
-            block(p, 2 * near + mine).start()
-        return carry
-
-    lax.fori_loop(0, ROWS, near_row, 0)
+    def group(first, count, dest, src):
+        part = pl.ds(first, count)
+        return pltpu.make_async_remote_copy(
+            src_ref=send.at[dest, part],
+            dst_ref=recv.at[src, part],
+            send_sem=send_sem.at[dest, first],
+            recv_sem=recv_sem.at[src, first],
+            device_id={"dev": dest},
+            device_id_type=pl.DeviceIdType.MESH,
+        )
+
+    @pl.when(is_edge)
+    def _():
+        def near_row(p, carry):
+            for mine in (core, 1 - core):
+                block(p, 2 * near + mine).start()
+            return carry
+
+        lax.fori_loop(0, ROWS, near_row, 0)
+
+    @pl.when(jnp.logical_not(is_edge))
+    def _():
+        for first, count in NEAR_GROUPS:
+            for mine in (core, 1 - core):
+                group(first, count, 2 * near + mine, me).start()
 
     c = c_vm[...]
     rows = lax.dot_general(spread, c, nt, preferred_element_type=F32)
@@ -158,15 +178,45 @@
         lax.fori_loop(0, ROWS // 2, body, 0)
 
     take([partner])
-    for other in (third_chip, far, near):
+    for other in (third_chip, far):
         take([2 * other, 2 * other + 1])
 
+    @pl.when(is_edge)
+    def _():
+        take([2 * near, 2 * near + 1])
+
+    @pl.when(jnp.logical_not(is_edge))
+    def _():
+        for first, count in NEAR_GROUPS:
+            for k in range(2):
+                src = 2 * near + k
+                group(first, count, src, src).wait_recv()
+                for p in range(first, first + count, 2):
+                    third(src, p, recv[src, p], recv[src, p + 1])
+
     def sent_row(p, carry):
-        for k in range(1, DEV):
-            block(p, (me + k) % DEV).wait_send()
+        block(p, partner).wait_send()
+        for other in (third_chip, far):
+            for k in range(2):
+                block(p, 2 * other + k).wait_send()
         return carry
 
     lax.fori_loop(0, ROWS, sent_row, 0)
+
+    @pl.when(is_edge)
+    def _():
+        def near_sent(p, carry):
+            for k in range(2):
+                block(p, 2 * near + k).wait_send()
+            return carry
+
+        lax.fori_loop(0, ROWS, near_sent, 0)
+
+    @pl.when(jnp.logical_not(is_edge))
+    def _():
+        for first, count in NEAR_GROUPS:
+            for k in range(2):
+                group(first, count, 2 * near + k, me).wait_send()
 
 
 def fourth_kernel(g_ref, l4_ref, v_hbm, v_vm, v_sem):

time: 101 us -> 100 us (0.990)
  no operation moved by 1% of the time
where the time goes in v8:
time: 100 us
  Pallas kernels  100 us (100%)
    pallas_call x1, Pallas kernels, local_transform(): pl.pallas_call(exchange_kernel, out_shape=(jax.ShapeDtypeStruct((8, 8 * N...  96.4 us
    pallas_call x1, Pallas kernels, local_transform(): pl.pallas_call(fourth_kernel, out_shape=jax.ShapeDtypeStruct((N, N, COLS)...  3.81 us

profile of v8, /device:TPU:15, one launch (start us, length us, event | category | flops | bytes accessed | tf_op | source)
XLA Modules:
  0.0 100.2 jit_solution(13508271502927579778)
XLA Ops:
  0.0 96.4 %exchange.1 = (bf16[8,512,512]{2,1,0:T(8,128)(2,1)S(1)}, bf16[512,512]{1,0:T(8,128)(2,1)S(1)}) custom-call(bf16[8,64,64,64]{3,2,1,0:T(8,128)(2,1)} %a_hbm.1, bf16[64,64]{1,0:T(8,128)(2,1)} %c_hbm.1), custom_call_target="tpu_custom_call" | custom-call | tf_op jit(solution)/shard_map/exchange/pallas_call | solution.py:237
  96.4 3.8 %fourth.1 = f32[64,64,512]{2,1,0:T(8,128)} custom-call(bf16[8,512,512]{2,1,0:T(8,128)(2,1)S(1)} %get-tuple-element.7.g_ref, bf16[512,512]{1,0:T(8,128)(2,1)S(1)} %get-tuple-element.8.l4_ref), custom_call_target="tpu_custom_call" | custom-call | tf_op jit(solution)/shard_map/fourth/pallas_call | solution.py:261

commit v9 on v7

--- a/solution.py
+++ b/solution.py
@@ -7,10 +7,12 @@
 from jax.experimental.pallas import tpu as pltpu
 from jax.sharding import PartitionSpec as P
 
+
 N = 64
 DEV = 8
 ROWS = N // DEV
 COLS = N * N // DEV
+CHUNKS = COLS // 128
 BF16 = jnp.bfloat16
 F32 = jnp.float32
 
@@ -19,7 +21,9 @@
     return lax.broadcasted_iota(jnp.int32, shape, dim)
 
 
-def exchange_kernel(a_hbm, c_hbm, g_ref, l4_ref, a_vm, c_vm, l_vm, b4_vm, ct_vm, send, recv, a_sem, c_sem, send_sem, recv_sem):
+def exchange_kernel(a_hbm, c_hbm, g_ref, l4_ref, l4n_ref, ct_ref, *refs):
+    near_refs = refs[:2 * CHUNKS]
+    a_vm, c_vm, l_vm, b4_vm, ct_vm, send, recv, a_sem, c_sem, send_sem, recv_sem = refs[2 * CHUNKS:]
     me = lax.axis_index("dev")
     chip = me // 2
     core = me % 2
@@ -90,7 +94,7 @@
     far = chip + 2 * inward
     last = chip + 3 * inward
     outward = chip - inward
-    third_chip = jnp.where(is_edge, last, outward)
+    beside = jnp.where(is_edge, near, outward)
 
     def make_row(p, carry):
         load_row(p).wait()
@@ -102,28 +106,42 @@
 
         for h in range(2):
             half_row(p, h)
-        for other in (third_chip, far):
-            for mine in (core, 1 - core):
-                block(p, 2 * other + mine).start()
+        for k in range(2):
+            block(p, 2 * beside + k).start()
+
+        @pl.when(jnp.logical_not(is_edge))
+        def _():
+            for k in range(2):
+                block(p, 2 * far + k).start()
+
         block(p, partner).start()
         return carry
 
     lax.fori_loop(0, ROWS, make_row, 0)
 
-    def near_row(p, carry):
-        for mine in (core, 1 - core):
-            block(p, 2 * near + mine).start()
-        return carry
-
-    lax.fori_loop(0, ROWS, near_row, 0)
+    @pl.when(is_edge)
+    def _():
+        for other in (far, last):
+            def far_row(p, carry):
+                for k in range(2):
+                    block(p, 2 * other + k).start()
+                return carry
+
+            lax.fori_loop(0, ROWS, far_row, 0)
+
+    for side, dest in ((0, 2 * near + core), (1, 2 * near + 1 - core)):
+        for chunk in range(CHUNKS):
+            near_refs[side * CHUNKS + chunk][...] = send[dest, :, :, pl.ds(128 * chunk, 128)]
 
     c = c_vm[...]
     rows = lax.dot_general(spread, c, nt, preferred_element_type=F32)
     widen = (iota((N, 8 * N), 0) == iota((N, 8 * N), 1) // 8).astype(BF16)
     full = jnp.dot(rows.astype(BF16), widen, preferred_element_type=F32)
     l4_ref[...] = jnp.where(iota(wide, 0) % 8 == iota(wide, 1) % 8, full, 0.0).astype(BF16)
+    l4n_ref[...] = l4_ref[:, pl.ds(pl.multiple_of(128 * near, 128), 128)]
     eye = (iota((N, N), 0) == iota((N, N), 1)).astype(BF16)
     ct_vm[...] = lax.dot_general(eye, c, nt, preferred_element_type=F32).astype(BF16)
+    ct_ref[...] = ct_vm[...]
 
     def third(src, p, first, second):
         g0 = jnp.dot(ct_vm[...], first, preferred_element_type=F32).reshape(8, 8, COLS)
@@ -158,23 +176,55 @@
         lax.fori_loop(0, ROWS // 2, body, 0)
 
     take([partner])
-    for other in (third_chip, far, near):
-        take([2 * other, 2 * other + 1])
+
+    @pl.when(jnp.logical_not(is_edge))
+    def _():
+        g_ref[:, pl.ds(pl.multiple_of(2 * N * near, 16), 2 * N), :] = jnp.zeros((8, 2 * N, COLS), BF16)
+
+    take([2 * beside, 2 * beside + 1])
+    take([2 * far, 2 * far + 1])
+
+    @pl.when(is_edge)
+    def _():
+        take([2 * last, 2 * last + 1])
 
     def sent_row(p, carry):
-        for k in range(1, DEV):
-            block(p, (me + k) % DEV).wait_send()
+        block(p, partner).wait_send()
+        for other in (beside, far):
+            for k in range(2):
+                block(p, 2 * other + k).wait_send()
+
+        @pl.when(is_edge)
+        def _():
+            for k in range(2):
+                block(p, 2 * last + k).wait_send()
+
         return carry
 
     lax.fori_loop(0, ROWS, sent_row, 0)
 
 
-def fourth_kernel(g_ref, l4_ref, v_hbm, v_vm, v_sem):
+def most_kernel(g_ref, l4_ref, v_ref):
+    for ag in range(8):
+        v_ref[ag] = jnp.dot(l4_ref[...], g_ref[ag], preferred_element_type=F32)
+
+
+def chunk_kernel(chunk, same_ref, other_ref, ct_ref, l4n_ref, most_ref, *refs):
+    v_hbm, g_vm, v_vm, v_sem = refs[-4:]
+    core = lax.axis_index("dev") % 2
+    for side, ref in ((core, same_ref), (1 - core, other_ref)):
+        for p in range(0, ROWS, 2):
+            g0 = jnp.dot(ct_ref[...], ref[p], preferred_element_type=F32).reshape(8, 8, 128)
+            g1 = jnp.dot(ct_ref[...], ref[p + 1], preferred_element_type=F32).reshape(8, 8, 128)
+            at = pl.multiple_of(N * side + 8 * p, 16)
+            g_vm[:, pl.ds(at, 16), :] = jnp.concatenate([g0, g1], axis=1).astype(BF16)
+
     def put(ag):
-        return pltpu.make_async_copy(v_vm.at[ag], v_hbm.at[:, pl.ds(8 * ag, 8), :], v_sem.at[ag])
+        return pltpu.make_async_copy(v_vm.at[ag], v_hbm.at[:, pl.ds(8 * ag, 8), pl.ds(128 * chunk, 128)], v_sem.at[ag])
 
     for ag in range(8):
-        v_vm[ag] = jnp.dot(l4_ref[...], g_ref[ag], preferred_element_type=F32).reshape(N, 8, COLS)
+        part = jnp.dot(l4n_ref[...], g_vm[ag], preferred_element_type=F32)
+        v_vm[ag] = (part + most_ref[ag, :, 128 * chunk:128 * chunk + 128]).reshape(N, 8, 128)
         put(ag).start()
     for ag in range(8):
         put(ag).wait()
@@ -184,14 +234,18 @@
     def local_transform(ao_rows, coeffs):
         vmem = pl.BlockSpec(memory_space=pltpu.VMEM)
         anywhere = pl.BlockSpec(memory_space=pltpu.HBM)
-        g, l4 = pl.pallas_call(
+        sds = jax.ShapeDtypeStruct
+        outs = (
+            sds((8, 8 * N, COLS), BF16),
+            sds((8 * N, 8 * N), BF16),
+            sds((8 * N, 2 * N), BF16),
+            sds((N, N), BF16),
+        ) + (sds((ROWS, N, 128), BF16),) * (2 * CHUNKS)
+        g, l4, l4n, ct, *near = pl.pallas_call(
             exchange_kernel,
-            out_shape=(
-                jax.ShapeDtypeStruct((8, 8 * N, COLS), BF16),
-                jax.ShapeDtypeStruct((8 * N, 8 * N), BF16),
-            ),
+            out_shape=outs,
             in_specs=[anywhere, anywhere],
-            out_specs=(vmem, vmem),
+            out_specs=(vmem,) * len(outs),
             scratch_shapes=[
                 pltpu.VMEM((ROWS, N, N, N), BF16),
                 pltpu.VMEM((N, N), BF16),
@@ -205,17 +259,43 @@
                 pltpu.SemaphoreType.DMA((DEV, ROWS)),
                 pltpu.SemaphoreType.DMA((DEV, ROWS)),
             ],
-            compiler_params=pltpu.CompilerParams(collective_id=0, has_side_effects=True, vmem_limit_bytes=48 * 2**20),
+            compiler_params=pltpu.CompilerParams(collective_id=0, has_side_effects=True, vmem_limit_bytes=40 * 2**20),
             name="exchange",
         )(pltpu.with_memory_space_constraint(ao_rows, pltpu.HBM), pltpu.with_memory_space_constraint(coeffs, pltpu.HBM))
-        return pl.pallas_call(
-            fourth_kernel,
-            out_shape=jax.ShapeDtypeStruct((N, N, COLS), F32),
+        same = [(2, 4), (3, 5), (4, 2), (5, 3)]
+        other = [(2, 5), (3, 4), (4, 3), (5, 2)]
+        arrived = []
+        for chunk in range(CHUNKS):
+            pair = []
+            for side, perm in enumerate((same, other)):
+                pair.append(lax.ppermute(near[side * CHUNKS + chunk], "dev", perm))
+            arrived.append(pair)
+        most = pl.pallas_call(
+            most_kernel,
+            out_shape=sds((8, 8 * N, COLS), F32),
             in_specs=[vmem, vmem],
-            out_specs=anywhere,
-            scratch_shapes=[pltpu.VMEM((8, N, 8, COLS), F32), pltpu.SemaphoreType.DMA((8,))],
-            compiler_params=pltpu.CompilerParams(vmem_limit_bytes=24 * 2**20),
-            name="fourth",
+            out_specs=vmem,
+            compiler_params=pltpu.CompilerParams(vmem_limit_bytes=12 * 2**20),
+            cost_estimate=pl.CostEstimate(flops=2 * 8 * 512**3, bytes_accessed=12 * 2**20, transcendentals=0),
+            name="most",
         )(g, l4)
+        v = None
+        for chunk in range(CHUNKS):
+            operands = (*arrived[chunk], ct, l4n, most) + (() if v is None else (v,))
+            v = pl.pallas_call(
+                functools.partial(chunk_kernel, chunk),
+                out_shape=sds((N, N, COLS), F32),
+                in_specs=[vmem] * 5 + ([] if v is None else [anywhere]),
+                out_specs=anywhere,
+                scratch_shapes=[
+                    pltpu.VMEM((8, 2 * N, 128), BF16),
+                    pltpu.VMEM((8, N, 8, 128), F32),
+                    pltpu.SemaphoreType.DMA((8,)),
+                ],
+                input_output_aliases={} if v is None else {5: 0},
+                compiler_params=pltpu.CompilerParams(vmem_limit_bytes=12 * 2**20),
+                cost_estimate=pl.CostEstimate(flops=2 * 8 * 512 * 128 * 128, bytes_accessed=4 * 2**20, transcendentals=0),
+            )(*operands)
+        return v
 
     return jax.shard_map(local_transform, mesh=mesh, in_specs=(P(('frag', 'dev')), P('frag')), out_specs=P('frag', None, 'dev'), check_vma=False)

time: 101 us -> 102 us (level)
  the two profiles are of different devices: /device:TPU:15 before, /device:TPU:23 now
where the time goes in v9:
time: 102 us
  Pallas kernels  62.9 us (62%)
  starting transfers between devices  20.5 us (20%)
  waiting for transfers between devices  18.1 us (18%)
    pallas_call x1, Pallas kernels, local_transform(): pl.pallas_call(exchange_kernel, out_shape=outs, in_specs=[anywhere, anywh...  53.2 us
    ppermute x8, starting transfers between devices, local_transform(): pair.append(lax.ppermute(near[side * CHUNKS + chunk], 'dev', perm))  20.5 us
    ppermute x8, waiting for transfers between devices, local_transform(): pair.append(lax.ppermute(near[side * CHUNKS + chunk], 'dev', perm))  18.1 us
    pallas_call x4, Pallas kernels, local_transform(): pl.pallas_call(functools.partial(chunk_kernel, chunk), out_shape=sds((N,...  7.33 us
    pallas_call x1, Pallas kernels, local_transform(): pl.pallas_call(most_kernel, out_shape=sds((8, 8 * N, COLS), F32), in_spec...  2.34 us
  transfers between devices with their start and end apart: 8, of which 3 were waited for; matrix products, arithmetic and copies ran while one was open for 0% of the time, Pallas kernels for 8%

profile of v9, /device:TPU:23, one launch (start us, length us, event | category | flops | bytes accessed | tf_op | source)
XLA Modules:
  0.0 101.7 jit_solution(15205623093951450411)
XLA Ops:
  0.0 53.2 %exchange.1 = (bf16[8,512,512]{2,1,0:T(8,128)(2,1)S(1)}, bf16[512,512]{1,0:T(8,128)(2,1)S(1)}, bf16[512,128]{1,0:T(8,128)(2,1)S(1)}, bf16[64,64]{1,0:T(8,128)(2,...) custom-call(bf16[8,64,64,64]{3,2,1,0:T(8,128)(2,1)} %a_hbm.1, ...), custom_call_target="tpu_custom_call" | custom-call | tf_op jit(solution)/shard_map/exchange/pallas_call | solution.py:244
  53.2 2.0 %collective-permute-start.4 = (bf16[8,64,128]{2,1,0:T(8,128)(2,1)S(1)}, bf16[8,64,128]{2,1,0:T(8,128)(2,1)S(1)}, u32[]{:S(2)}, u32[]{:S(2)}) collective-permute-start(bf16[8,64,128]{2,1,0:T(8,128)(2,1)S(1)} %get-tuple-element.25), channel_id=1, source_target_pairs={{2,4},{3,5},{4,2},{5,3},{10,12},{11,13},{12,10},{13,11},{18,20},{1... | collective-permute-start | bytes 393224 | tf_op jit(solution)/shard_map/ppermute | solution.py:271
  55.2 3.3 %collective-permute-start.6 = (bf16[8,64,128]{2,1,0:T(8,128)(2,1)S(1)}, bf16[8,64,128]{2,1,0:T(8,128)(2,1)S(1)}, u32[]{:S(2)}, u32[]{:S(2)}) collective-permute-start(bf16[8,64,128]{2,1,0:T(8,128)(2,1)S(1)} %get-tuple-element.27), channel_id=1, source_target_pairs={{2,4},{3,5},{4,2},{5,3},{10,12},{11,13},{12,10},{13,11},{18,20},{1... | collective-permute-start | bytes 393224 | tf_op jit(solution)/shard_map/ppermute | solution.py:271
  58.5 1.9 %collective-permute-start.7 = (bf16[8,64,128]{2,1,0:T(8,128)(2,1)S(1)}, bf16[8,64,128]{2,1,0:T(8,128)(2,1)S(1)}, u32[]{:S(2)}, u32[]{:S(2)}) collective-permute-start(bf16[8,64,128]{2,1,0:T(8,128)(2,1)S(1)} %get-tuple-element.28), channel_id=1, source_target_pairs={{2,5},{3,4},{4,3},{5,2},{10,13},{11,12},{12,11},{13,10},{18,21},{1... | collective-permute-start | bytes 393224 | tf_op jit(solution)/shard_map/ppermute | solution.py:271
  60.4 3.1 %collective-permute-start = (bf16[8,64,128]{2,1,0:T(8,128)(2,1)S(1)}, bf16[8,64,128]{2,1,0:T(8,128)(2,1)S(1)}, u32[]{:S(2)}, u32[]{:S(2)}) collective-permute-start(bf16[8,64,128]{2,1,0:T(8,128)(2,1)S(1)} %get-tuple-element.17), channel_id=1, source_target_pairs={{2,4},{3,5},{4,2},{5,3},{10,12},{11,13},{12,10},{13,11},{18,20},{1... | collective-permute-start | bytes 393224 | tf_op jit(solution)/shard_map/ppermute | solution.py:271
  63.5 2.8 %collective-permute-start.1 = (bf16[8,64,128]{2,1,0:T(8,128)(2,1)S(1)}, bf16[8,64,128]{2,1,0:T(8,128)(2,1)S(1)}, u32[]{:S(2)}, u32[]{:S(2)}) collective-permute-start(bf16[8,64,128]{2,1,0:T(8,128)(2,1)S(1)} %get-tuple-element.18), channel_id=1, source_target_pairs={{2,5},{3,4},{4,3},{5,2},{10,13},{11,12},{12,11},{13,10},{18,21},{1... | collective-permute-start | bytes 393224 | tf_op jit(solution)/shard_map/ppermute | solution.py:271
  66.3 10.2 %collective-permute-done.4.same_ref = bf16[8,64,128]{2,1,0:T(8,128)(2,1)S(1)} collective-permute-done((bf16[8,64,128]{2,1,0:T(8,128)(2,1)S(1)}, bf16[8,64,128]{2,1,0:T(8,128)(2,1)S(1)}, u32[]{:S(2)}, u32[]{:S(2)}) %collective-permute-start.4) | collective-permute-done | bytes 131104 | tf_op jit(solution)/shard_map/ppermute | solution.py:271
  76.5 1.9 %collective-permute-start.2 = (bf16[8,64,128]{2,1,0:T(8,128)(2,1)S(1)}, bf16[8,64,128]{2,1,0:T(8,128)(2,1)S(1)}, u32[]{:S(2)}, u32[]{:S(2)}) collective-permute-start(bf16[8,64,128]{2,1,0:T(8,128)(2,1)S(1)} %get-tuple-element.23), channel_id=1, source_target_pairs={{2,4},{3,5},{4,2},{5,3},{10,12},{11,13},{12,10},{13,11},{18,20},{1... | collective-permute-start | bytes 393224 | tf_op jit(solution)/shard_map/ppermute | solution.py:271
  78.4 0.9 collective-permute-done.6.same_ref
  79.3 3.0 %collective-permute-start.3 = (bf16[8,64,128]{2,1,0:T(8,128)(2,1)S(1)}, bf16[8,64,128]{2,1,0:T(8,128)(2,1)S(1)}, u32[]{:S(2)}, u32[]{:S(2)}) collective-permute-start(bf16[8,64,128]{2,1,0:T(8,128)(2,1)S(1)} %get-tuple-element.24), channel_id=1, source_target_pairs={{2,5},{3,4},{4,3},{5,2},{10,13},{11,12},{12,11},{13,10},{18,21},{1... | collective-permute-start | bytes 393224 | tf_op jit(solution)/shard_map/ppermute | solution.py:271
  82.3 0.0 collective-permute-done.7.other_ref
  82.3 2.5 %collective-permute-start.5 = (bf16[8,64,128]{2,1,0:T(8,128)(2,1)S(1)}, bf16[8,64,128]{2,1,0:T(8,128)(2,1)S(1)}, u32[]{:S(2)}, u32[]{:S(2)}) collective-permute-start(bf16[8,64,128]{2,1,0:T(8,128)(2,1)S(1)} %get-tuple-element.26), channel_id=1, source_target_pairs={{2,5},{3,4},{4,3},{5,2},{10,13},{11,12},{12,11},{13,10},{18,21},{1... | collective-permute-start | bytes 393224 | tf_op jit(solution)/shard_map/ppermute | solution.py:271
  84.9 2.3 %most.1.most_ref = f32[8,512,512]{2,1,0:T(8,128)S(1)} custom-call(bf16[8,512,512]{2,1,0:T(8,128)(2,1)S(1)} %get-tuple-element.21.g_ref, bf16[512,512]{1,0:T(8,128)(2,1)S(1)} %get-tuple-element.22.l4_ref), custom_call_target="tpu_custom_call" | custom-call | flops 2147483648 | bytes 12582912 | tf_op jit(solution)/shard_map/most/pallas_call | solution.py:273
  87.2 1.8 %shard_map.28.refs_0_ = f32[64,64,512]{2,1,0:T(8,128)} custom-call(bf16[8,64,128]{2,1,0:T(8,128)(2,1)S(1)} %collective-permute-done.6.same_ref, bf16[8,64,128]{2,1,0:T(8,128)(2,1)S(1)} %collective-permute-done.7.other_ref, bf16[64,64]{1,0:T(8,128)(2,1)S(1)} %get-tuple-element.19.ct_ref, bf16[512,128]{1,0:T(8,128)(2,1)S(1)} %get-tuple-element.20.l4n_ref, ...), custom_call_target="tpu_custom_call" | custom-call | flops 134217728 | bytes 4194304 | tf_op jit(solution)/shard_map/pallas_call | solution.py:285
  89.0 7.1 %collective-permute-done.5.other_ref = bf16[8,64,128]{2,1,0:T(8,128)(2,1)S(1)} collective-permute-done((bf16[8,64,128]{2,1,0:T(8,128)(2,1)S(1)}, bf16[8,64,128]{2,1,0:T(8,128)(2,1)S(1)}, u32[]{:S(2)}, u32[]{:S(2)}) %collective-permute-start.5) | collective-permute-done | bytes 131104 | tf_op jit(solution)/shard_map/ppermute | solution.py:271
  96.1 1.8 %shard_map.29.refs_0_ = f32[64,64,512]{2,1,0:T(8,128)} custom-call(bf16[8,64,128]{2,1,0:T(8,128)(2,1)S(1)} %collective-permute-done.4.same_ref, bf16[8,64,128]{2,1,0:T(8,128)(2,1)S(1)} %collective-permute-done.5.other_ref, bf16[64,64]{1,0:T(8,128)(2,1)S(1)} %get-tuple-element.19.ct_ref, ...), custom_call_target="tpu_custom_call", output_to_operand_aliasing={{}: (5, {})} | custom-call | flops 134217728 | bytes 4194304 | tf_op jit(solution)/shard_map/pallas_call | solution.py:285
  98.0 0.0 collective-permute-done.2.same_ref
  98.0 0.0 collective-permute-done.3.other_ref
  98.0 1.8 %shard_map.30.refs_0_ = f32[64,64,512]{2,1,0:T(8,128)} custom-call(bf16[8,64,128]{2,1,0:T(8,128)(2,1)S(1)} %collective-permute-done.2.same_ref, bf16[8,64,128]{2,1,0:T(8,128)(2,1)S(1)} %collective-permute-done.3.other_ref, bf16[64,64]{1,0:T(8,128)(2,1)S(1)} %get-tuple-element.19.ct_ref, ...), custom_call_target="tpu_custom_call", output_to_operand_aliasing={{}: (5, {})} | custom-call | flops 134217728 | bytes 4194304 | tf_op jit(solution)/shard_map/pallas_call | solution.py:285
  99.8 0.0 collective-permute-done.same_ref
  99.8 0.0 collective-permute-done.1.other_ref
  99.9 1.8 %shard_map.31 = f32[64,64,512]{2,1,0:T(8,128)} custom-call(bf16[8,64,128]{2,1,0:T(8,128)(2,1)S(1)} %collective-permute-done.same_ref, bf16[8,64,128]{2,1,0:T(8,128)(2,1)S(1)} %collective-permute-done.1.other_ref, bf16[64,64]{1,0:T(8,128)(2,1)S(1)} %get-tuple-element.19.ct_ref, ...), custom_call_target="tpu_custom_call", output_to_operand_aliasing={{}: (5, {})} | custom-call | flops 134217728 | bytes 4194304 | tf_op jit(solution)/shard_map/pallas_call | solution.py:285
Async XLA Ops:
  53.2 23.3 %collective-permute-start.4 = (bf16[8,64,128]{2,1,0:T(8,128)(2,1)S(1)}, bf16[8,64,128]{2,1,0:T(8,128)(2,1)S(1)}, u32[]{:S(2)}, u32[]{:S(2)}) collective-permute-start(bf16[8,64,128]{2,1,0:T(8,128)(2,1)S(1)} %get-tuple-element.25), channel_id=1, source_target_pairs={{2,4},{3,5},{4,2},{5,3},{10,12},{11,13},{12,10},{13,11},{18,20},{1... | collective-permute-start | bytes 393224 | tf_op jit(solution)/shard_map/ppermute | solution.py:271
  55.2 24.1 %collective-permute-start.6 = (bf16[8,64,128]{2,1,0:T(8,128)(2,1)S(1)}, bf16[8,64,128]{2,1,0:T(8,128)(2,1)S(1)}, u32[]{:S(2)}, u32[]{:S(2)}) collective-permute-start(bf16[8,64,128]{2,1,0:T(8,128)(2,1)S(1)} %get-tuple-element.27), channel_id=1, source_target_pairs={{2,4},{3,5},{4,2},{5,3},{10,12},{11,13},{12,10},{13,11},{18,20},{1... | collective-permute-start | bytes 393224 | tf_op jit(solution)/shard_map/ppermute | solution.py:271
  58.5 23.8 %collective-permute-start.7 = (bf16[8,64,128]{2,1,0:T(8,128)(2,1)S(1)}, bf16[8,64,128]{2,1,0:T(8,128)(2,1)S(1)}, u32[]{:S(2)}, u32[]{:S(2)}) collective-permute-start(bf16[8,64,128]{2,1,0:T(8,128)(2,1)S(1)} %get-tuple-element.28), channel_id=1, source_target_pairs={{2,5},{3,4},{4,3},{5,2},{10,13},{11,12},{12,11},{13,10},{18,21},{1... | collective-permute-start | bytes 393224 | tf_op jit(solution)/shard_map/ppermute | solution.py:271
  60.4 39.4 %collective-permute-start = (bf16[8,64,128]{2,1,0:T(8,128)(2,1)S(1)}, bf16[8,64,128]{2,1,0:T(8,128)(2,1)S(1)}, u32[]{:S(2)}, u32[]{:S(2)}) collective-permute-start(bf16[8,64,128]{2,1,0:T(8,128)(2,1)S(1)} %get-tuple-element.17), channel_id=1, source_target_pairs={{2,4},{3,5},{4,2},{5,3},{10,12},{11,13},{12,10},{13,11},{18,20},{1... | collective-permute-start | bytes 393224 | tf_op jit(solution)/shard_map/ppermute | solution.py:271
  63.5 36.3 %collective-permute-start.1 = (bf16[8,64,128]{2,1,0:T(8,128)(2,1)S(1)}, bf16[8,64,128]{2,1,0:T(8,128)(2,1)S(1)}, u32[]{:S(2)}, u32[]{:S(2)}) collective-permute-start(bf16[8,64,128]{2,1,0:T(8,128)(2,1)S(1)} %get-tuple-element.18), channel_id=1, source_target_pairs={{2,5},{3,4},{4,3},{5,2},{10,13},{11,12},{12,11},{13,10},{18,21},{1... | collective-permute-start | bytes 393224 | tf_op jit(solution)/shard_map/ppermute | solution.py:271
  76.5 21.5 %collective-permute-start.2 = (bf16[8,64,128]{2,1,0:T(8,128)(2,1)S(1)}, bf16[8,64,128]{2,1,0:T(8,128)(2,1)S(1)}, u32[]{:S(2)}, u32[]{:S(2)}) collective-permute-start(bf16[8,64,128]{2,1,0:T(8,128)(2,1)S(1)} %get-tuple-element.23), channel_id=1, source_target_pairs={{2,4},{3,5},{4,2},{5,3},{10,12},{11,13},{12,10},{13,11},{18,20},{1... | collective-permute-start | bytes 393224 | tf_op jit(solution)/shard_map/ppermute | solution.py:271
  79.3 18.7 %collective-permute-start.3 = (bf16[8,64,128]{2,1,0:T(8,128)(2,1)S(1)}, bf16[8,64,128]{2,1,0:T(8,128)(2,1)S(1)}, u32[]{:S(2)}, u32[]{:S(2)}) collective-permute-start(bf16[8,64,128]{2,1,0:T(8,128)(2,1)S(1)} %get-tuple-element.24), channel_id=1, source_target_pairs={{2,5},{3,4},{4,3},{5,2},{10,13},{11,12},{12,11},{13,10},{18,21},{1... | collective-permute-start | bytes 393224 | tf_op jit(solution)/shard_map/ppermute | solution.py:271
  82.3 13.8 %collective-permute-start.5 = (bf16[8,64,128]{2,1,0:T(8,128)(2,1)S(1)}, bf16[8,64,128]{2,1,0:T(8,128)(2,1)S(1)}, u32[]{:S(2)}, u32[]{:S(2)}) collective-permute-start(bf16[8,64,128]{2,1,0:T(8,128)(2,1)S(1)} %get-tuple-element.26), channel_id=1, source_target_pairs={{2,5},{3,4},{4,3},{5,2},{10,13},{11,12},{12,11},{13,10},{18,21},{1... | collective-permute-start | bytes 393224 | tf_op jit(solution)/shard_map/ppermute | solution.py:271

commit v10 on v9

--- a/solution.py
+++ b/solution.py
@@ -34,7 +34,12 @@
     def load_row(p):
         return pltpu.make_async_copy(a_hbm.at[p], a_vm.at[p], a_sem.at[p])
 
-    load_row(0).start()
+    def load_half(h):
+        half = pl.ds(32 * h, 32)
+        return pltpu.make_async_copy(a_hbm.at[0, half], a_vm.at[0, half], a_sem.at[ROWS * h])
+
+    for h in range(2):
+        load_half(h).start()
 
     barrier = pltpu.get_barrier_semaphore()
     for k in range(1, DEV):
@@ -70,22 +75,36 @@
 
     low = iota((32, 8, 128), 2) < N
 
-    def half_row(p, h):
+    def pieces(p, h, first, count, put):
         a = a_vm[p, pl.ds(32 * h, 32)].reshape(4, 8 * N, N)
         left = jnp.concatenate([a[0], a[1]], axis=1)
         right = jnp.concatenate([a[2], a[3]], axis=1)
         a4 = jnp.concatenate([left, right], axis=1)
-        t_one = jnp.dot(l_vm[...], a4, preferred_element_type=F32).astype(BF16)
+        lhs = l_vm[pl.ds(first, 16 * count), :]
+        t_one = jnp.dot(lhs, a4, preferred_element_type=F32).astype(BF16)
         half = jnp.dot(t_one, b4_vm[...], preferred_element_type=F32)
-        pairs = half.reshape(32, 2, 8, 256)
+        pairs = half.reshape(count, 2, 8, 256)
         for t in range(2):
             even = pairs[:, 0, :, 128 * t:128 * t + 128]
             odd = pairs[:, 1, :, 128 * t:128 * t + 128]
-            first = jnp.where(low, even, pltpu.roll(odd, N, 2))
-            second = jnp.where(low, pltpu.roll(even, N, 2), odd)
-            both = jnp.concatenate([first, second], axis=1).astype(BF16)
-            for jp in range(32):
-                send[jp // 4, p, pl.ds(32 * h + 16 * t, 16), pl.ds(128 * (jp % 4), 128)] = both[jp]
+            first_rows = jnp.where(low[:count], even, pltpu.roll(odd, N, 2))
+            second_rows = jnp.where(low[:count], pltpu.roll(even, N, 2), odd)
+            both = jnp.concatenate([first_rows, second_rows], axis=1).astype(BF16)
+            for jp in range(count):
+                put(jp // 4, pl.ds(32 * h + 16 * t, 16), pl.ds(128 * (jp % 4), 128), both[jp])
+
+    def half_row(p, h):
+        def put(dest, q, columns, value):
+            send[dest, p, q, columns] = value
+
+        pieces(p, h, 0, 32, put)
+
+    def chip_piece(to):
+        def put(dest, q, columns, value):
+            send[2 * to + dest, 0, q, columns] = value
+
+        for h in range(2):
+            pieces(0, h, pl.multiple_of(128 * to, 128), 8, put)
 
     is_edge = jnp.logical_or(chip == 0, chip == 3)
     inward = jnp.where(chip < 2, 1, -1)
@@ -96,14 +115,26 @@
     outward = chip - inward
     beside = jnp.where(is_edge, near, outward)
 
+    for h in range(2):
+        load_half(h).wait()
+    for later in range(1, ROWS):
+        load_row(later).start()
+    chip_piece(jnp.where(is_edge, near, far))
+    for k in range(2):
+        block(0, 2 * jnp.where(is_edge, near, far) + k).start()
+    chip_piece(jnp.where(is_edge, far, outward))
+
+    @pl.when(jnp.logical_not(is_edge))
+    def _():
+        for k in range(2):
+            block(0, 2 * outward + k).start()
+
+    chip_piece(jnp.where(is_edge, last, near))
+    chip_piece(chip)
+    block(0, partner).start()
+
     def make_row(p, carry):
         load_row(p).wait()
-
-        @pl.when(p == 0)
-        def _():
-            for later in range(1, ROWS):
-                load_row(later).start()
-
         for h in range(2):
             half_row(p, h)
         for k in range(2):
@@ -117,7 +148,7 @@
         block(p, partner).start()
         return carry
 
-    lax.fori_loop(0, ROWS, make_row, 0)
+    lax.fori_loop(1, ROWS, make_row, 0)
 
     @pl.when(is_edge)
     def _():
@@ -214,18 +245,24 @@
     core = lax.axis_index("dev") % 2
     for side, ref in ((core, same_ref), (1 - core, other_ref)):
         for p in range(0, ROWS, 2):
-            g0 = jnp.dot(ct_ref[...], ref[p], preferred_element_type=F32).reshape(8, 8, 128)
-            g1 = jnp.dot(ct_ref[...], ref[p + 1], preferred_element_type=F32).reshape(8, 8, 128)
+            both = jnp.concatenate([ref[p], ref[p + 1]], axis=1)
+            g = jnp.dot(ct_ref[...], both, preferred_element_type=F32)
+            g0 = g[:, :128].reshape(8, 8, 128)
+            g1 = g[:, 128:].reshape(8, 8, 128)
+            g = jnp.concatenate([g0, g1], axis=1).astype(BF16)
             at = pl.multiple_of(N * side + 8 * p, 16)
-            g_vm[:, pl.ds(at, 16), :] = jnp.concatenate([g0, g1], axis=1).astype(BF16)
+            for ag in range(8):
+                g_vm[pl.ds(at, 16), 128 * ag:128 * ag + 128] = g[ag]
 
     def put(ag):
         return pltpu.make_async_copy(v_vm.at[ag], v_hbm.at[:, pl.ds(8 * ag, 8), pl.ds(128 * chunk, 128)], v_sem.at[ag])
 
-    for ag in range(8):
-        part = jnp.dot(l4n_ref[...], g_vm[ag], preferred_element_type=F32)
-        v_vm[ag] = (part + most_ref[ag, :, 128 * chunk:128 * chunk + 128]).reshape(N, 8, 128)
-        put(ag).start()
+    for pair in range(4):
+        part = jnp.dot(l4n_ref[...], g_vm[:, 256 * pair:256 * pair + 256], preferred_element_type=F32)
+        for k in range(2):
+            ag = 2 * pair + k
+            v_vm[ag] = (part[:, 128 * k:128 * k + 128] + most_ref[ag, :, 128 * chunk:128 * chunk + 128]).reshape(N, 8, 128)
+            put(ag).start()
     for ag in range(8):
         put(ag).wait()
 
@@ -254,7 +291,7 @@
                 pltpu.VMEM((N, N), BF16),
                 pltpu.VMEM((DEV, ROWS, N, COLS), BF16),
                 pltpu.VMEM((DEV, ROWS, N, COLS), BF16),
-                pltpu.SemaphoreType.DMA((ROWS,)),
+                pltpu.SemaphoreType.DMA((ROWS + 1,)),
                 pltpu.SemaphoreType.DMA,
                 pltpu.SemaphoreType.DMA((DEV, ROWS)),
                 pltpu.SemaphoreType.DMA((DEV, ROWS)),
@@ -288,7 +325,7 @@
                 in_specs=[vmem] * 5 + ([] if v is None else [anywhere]),
                 out_specs=anywhere,
                 scratch_shapes=[
-                    pltpu.VMEM((8, 2 * N, 128), BF16),
+                    pltpu.VMEM((2 * N, 8 * 128), BF16),
                     pltpu.VMEM((8, N, 8, 128), F32),
                     pltpu.SemaphoreType.DMA((8,)),
                 ],

time: 102 us -> 102 us (level)
  the two profiles are of different devices: /device:TPU:23 before, /device:TPU:21 now
where the time goes in v10:
time: 102 us
  Pallas kernels  62.9 us (62%)
  starting transfers between devices  20.5 us (20%)
  waiting for transfers between devices  18 us (18%)
    pallas_call x1, Pallas kernels, local_transform(): pl.pallas_call(exchange_kernel, out_shape=outs, in_specs=[anywhere, anywh...  52.7 us
    ppermute x8, starting transfers between devices, local_transform(): pair.append(lax.ppermute(near[side * CHUNKS + chunk], 'dev', perm))  20.5 us
    ppermute x8, waiting for transfers between devices, local_transform(): pair.append(lax.ppermute(near[side * CHUNKS + chunk], 'dev', perm))  18 us
    pallas_call x4, Pallas kernels, local_transform(): pl.pallas_call(functools.partial(chunk_kernel, chunk), out_shape=sds((N,...  7.88 us
    pallas_call x1, Pallas kernels, local_transform(): pl.pallas_call(most_kernel, out_shape=sds((8, 8 * N, COLS), F32), in_spec...  2.34 us
  transfers between devices with their start and end apart: 8, of which 3 were waited for; matrix products, arithmetic and copies ran while one was open for 0% of the time, Pallas kernels for 8%

profile of v10, /device:TPU:21, one launch (start us, length us, event | category | flops | bytes accessed | tf_op | source)
XLA Modules:
  0.0 101.6 jit_solution(17609618246981180346)
XLA Ops:
  0.0 52.7 %exchange.1 = (bf16[8,512,512]{2,1,0:T(8,128)(2,1)S(1)}, bf16[512,512]{1,0:T(8,128)(2,1)S(1)}, bf16[512,128]{1,0:T(8,128)(2,1)S(1)}, bf16[64,64]{1,0:T(8,128)(2,...) custom-call(bf16[8,64,64,64]{3,2,1,0:T(8,128)(2,1)} %a_hbm.1, ...), custom_call_target="tpu_custom_call" | custom-call | tf_op jit(solution)/shard_map/exchange/pallas_call | solution.py:281
  52.7 2.0 %collective-permute-start.4 = (bf16[8,64,128]{2,1,0:T(8,128)(2,1)S(1)}, bf16[8,64,128]{2,1,0:T(8,128)(2,1)S(1)}, u32[]{:S(2)}, u32[]{:S(2)}) collective-permute-start(bf16[8,64,128]{2,1,0:T(8,128)(2,1)S(1)} %get-tuple-element.25), channel_id=1, source_target_pairs={{2,4},{3,5},{4,2},{5,3},{10,12},{11,13},{12,10},{13,11},{18,20},{1... | collective-permute-start | bytes 393224 | tf_op jit(solution)/shard_map/ppermute | solution.py:308
  54.7 3.3 %collective-permute-start.6 = (bf16[8,64,128]{2,1,0:T(8,128)(2,1)S(1)}, bf16[8,64,128]{2,1,0:T(8,128)(2,1)S(1)}, u32[]{:S(2)}, u32[]{:S(2)}) collective-permute-start(bf16[8,64,128]{2,1,0:T(8,128)(2,1)S(1)} %get-tuple-element.27), channel_id=1, source_target_pairs={{2,4},{3,5},{4,2},{5,3},{10,12},{11,13},{12,10},{13,11},{18,20},{1... | collective-permute-start | bytes 393224 | tf_op jit(solution)/shard_map/ppermute | solution.py:308
  58.0 1.9 %collective-permute-start.7 = (bf16[8,64,128]{2,1,0:T(8,128)(2,1)S(1)}, bf16[8,64,128]{2,1,0:T(8,128)(2,1)S(1)}, u32[]{:S(2)}, u32[]{:S(2)}) collective-permute-start(bf16[8,64,128]{2,1,0:T(8,128)(2,1)S(1)} %get-tuple-element.28), channel_id=1, source_target_pairs={{2,5},{3,4},{4,3},{5,2},{10,13},{11,12},{12,11},{13,10},{18,21},{1... | collective-permute-start | bytes 393224 | tf_op jit(solution)/shard_map/ppermute | solution.py:308
  59.9 3.1 %collective-permute-start = (bf16[8,64,128]{2,1,0:T(8,128)(2,1)S(1)}, bf16[8,64,128]{2,1,0:T(8,128)(2,1)S(1)}, u32[]{:S(2)}, u32[]{:S(2)}) collective-permute-start(bf16[8,64,128]{2,1,0:T(8,128)(2,1)S(1)} %get-tuple-element.17), channel_id=1, source_target_pairs={{2,4},{3,5},{4,2},{5,3},{10,12},{11,13},{12,10},{13,11},{18,20},{1... | collective-permute-start | bytes 393224 | tf_op jit(solution)/shard_map/ppermute | solution.py:308
  63.0 2.8 %collective-permute-start.1 = (bf16[8,64,128]{2,1,0:T(8,128)(2,1)S(1)}, bf16[8,64,128]{2,1,0:T(8,128)(2,1)S(1)}, u32[]{:S(2)}, u32[]{:S(2)}) collective-permute-start(bf16[8,64,128]{2,1,0:T(8,128)(2,1)S(1)} %get-tuple-element.18), channel_id=1, source_target_pairs={{2,5},{3,4},{4,3},{5,2},{10,13},{11,12},{12,11},{13,10},{18,21},{1... | collective-permute-start | bytes 393224 | tf_op jit(solution)/shard_map/ppermute | solution.py:308
  65.8 10.2 %collective-permute-done.4.same_ref = bf16[8,64,128]{2,1,0:T(8,128)(2,1)S(1)} collective-permute-done((bf16[8,64,128]{2,1,0:T(8,128)(2,1)S(1)}, bf16[8,64,128]{2,1,0:T(8,128)(2,1)S(1)}, u32[]{:S(2)}, u32[]{:S(2)}) %collective-permute-start.4) | collective-permute-done | bytes 131104 | tf_op jit(solution)/shard_map/ppermute | solution.py:308
  76.0 1.9 %collective-permute-start.2 = (bf16[8,64,128]{2,1,0:T(8,128)(2,1)S(1)}, bf16[8,64,128]{2,1,0:T(8,128)(2,1)S(1)}, u32[]{:S(2)}, u32[]{:S(2)}) collective-permute-start(bf16[8,64,128]{2,1,0:T(8,128)(2,1)S(1)} %get-tuple-element.23), channel_id=1, source_target_pairs={{2,4},{3,5},{4,2},{5,3},{10,12},{11,13},{12,10},{13,11},{18,20},{1... | collective-permute-start | bytes 393224 | tf_op jit(solution)/shard_map/ppermute | solution.py:308
  77.9 0.9 collective-permute-done.6.same_ref
  78.7 3.0 %collective-permute-start.3 = (bf16[8,64,128]{2,1,0:T(8,128)(2,1)S(1)}, bf16[8,64,128]{2,1,0:T(8,128)(2,1)S(1)}, u32[]{:S(2)}, u32[]{:S(2)}) collective-permute-start(bf16[8,64,128]{2,1,0:T(8,128)(2,1)S(1)} %get-tuple-element.24), channel_id=1, source_target_pairs={{2,5},{3,4},{4,3},{5,2},{10,13},{11,12},{12,11},{13,10},{18,21},{1... | collective-permute-start | bytes 393224 | tf_op jit(solution)/shard_map/ppermute | solution.py:308
  81.8 0.0 collective-permute-done.7.other_ref
  81.8 2.5 %collective-permute-start.5 = (bf16[8,64,128]{2,1,0:T(8,128)(2,1)S(1)}, bf16[8,64,128]{2,1,0:T(8,128)(2,1)S(1)}, u32[]{:S(2)}, u32[]{:S(2)}) collective-permute-start(bf16[8,64,128]{2,1,0:T(8,128)(2,1)S(1)} %get-tuple-element.26), channel_id=1, source_target_pairs={{2,5},{3,4},{4,3},{5,2},{10,13},{11,12},{12,11},{13,10},{18,21},{1... | collective-permute-start | bytes 393224 | tf_op jit(solution)/shard_map/ppermute | solution.py:308
  84.3 2.3 %most.1.most_ref = f32[8,512,512]{2,1,0:T(8,128)S(1)} custom-call(bf16[8,512,512]{2,1,0:T(8,128)(2,1)S(1)} %get-tuple-element.21.g_ref, bf16[512,512]{1,0:T(8,128)(2,1)S(1)} %get-tuple-element.22.l4_ref), custom_call_target="tpu_custom_call" | custom-call | flops 2147483648 | bytes 12582912 | tf_op jit(solution)/shard_map/most/pallas_call | solution.py:310
  86.7 2.0 %shard_map.28.refs_0_ = f32[64,64,512]{2,1,0:T(8,128)} custom-call(bf16[8,64,128]{2,1,0:T(8,128)(2,1)S(1)} %collective-permute-done.6.same_ref, bf16[8,64,128]{2,1,0:T(8,128)(2,1)S(1)} %collective-permute-done.7.other_ref, bf16[64,64]{1,0:T(8,128)(2,1)S(1)} %get-tuple-element.19.ct_ref, bf16[512,128]{1,0:T(8,128)(2,1)S(1)} %get-tuple-element.20.l4n_ref, ...), custom_call_target="tpu_custom_call" | custom-call | flops 134217728 | bytes 4194304 | tf_op jit(solution)/shard_map/pallas_call | solution.py:322
  88.7 6.9 %collective-permute-done.5.other_ref = bf16[8,64,128]{2,1,0:T(8,128)(2,1)S(1)} collective-permute-done((bf16[8,64,128]{2,1,0:T(8,128)(2,1)S(1)}, bf16[8,64,128]{2,1,0:T(8,128)(2,1)S(1)}, u32[]{:S(2)}, u32[]{:S(2)}) %collective-permute-start.5) | collective-permute-done | bytes 131104 | tf_op jit(solution)/shard_map/ppermute | solution.py:308
  95.6 2.0 %shard_map.29.refs_0_ = f32[64,64,512]{2,1,0:T(8,128)} custom-call(bf16[8,64,128]{2,1,0:T(8,128)(2,1)S(1)} %collective-permute-done.4.same_ref, bf16[8,64,128]{2,1,0:T(8,128)(2,1)S(1)} %collective-permute-done.5.other_ref, bf16[64,64]{1,0:T(8,128)(2,1)S(1)} %get-tuple-element.19.ct_ref, ...), custom_call_target="tpu_custom_call", output_to_operand_aliasing={{}: (5, {})} | custom-call | flops 134217728 | bytes 4194304 | tf_op jit(solution)/shard_map/pallas_call | solution.py:322
  97.6 0.0 collective-permute-done.2.same_ref
  97.6 0.0 collective-permute-done.3.other_ref
  97.6 2.0 %shard_map.30.refs_0_ = f32[64,64,512]{2,1,0:T(8,128)} custom-call(bf16[8,64,128]{2,1,0:T(8,128)(2,1)S(1)} %collective-permute-done.2.same_ref, bf16[8,64,128]{2,1,0:T(8,128)(2,1)S(1)} %collective-permute-done.3.other_ref, bf16[64,64]{1,0:T(8,128)(2,1)S(1)} %get-tuple-element.19.ct_ref, ...), custom_call_target="tpu_custom_call", output_to_operand_aliasing={{}: (5, {})} | custom-call | flops 134217728 | bytes 4194304 | tf_op jit(solution)/shard_map/pallas_call | solution.py:322
  99.6 0.0 collective-permute-done.same_ref
  99.6 0.0 collective-permute-done.1.other_ref
  99.6 2.0 %shard_map.31 = f32[64,64,512]{2,1,0:T(8,128)} custom-call(bf16[8,64,128]{2,1,0:T(8,128)(2,1)S(1)} %collective-permute-done.same_ref, bf16[8,64,128]{2,1,0:T(8,128)(2,1)S(1)} %collective-permute-done.1.other_ref, bf16[64,64]{1,0:T(8,128)(2,1)S(1)} %get-tuple-element.19.ct_ref, ...), custom_call_target="tpu_custom_call", output_to_operand_aliasing={{}: (5, {})} | custom-call | flops 134217728 | bytes 4194304 | tf_op jit(solution)/shard_map/pallas_call | solution.py:322
Async XLA Ops:
  52.7 23.3 %collective-permute-start.4 = (bf16[8,64,128]{2,1,0:T(8,128)(2,1)S(1)}, bf16[8,64,128]{2,1,0:T(8,128)(2,1)S(1)}, u32[]{:S(2)}, u32[]{:S(2)}) collective-permute-start(bf16[8,64,128]{2,1,0:T(8,128)(2,1)S(1)} %get-tuple-element.25), channel_id=1, source_target_pairs={{2,4},{3,5},{4,2},{5,3},{10,12},{11,13},{12,10},{13,11},{18,20},{1... | collective-permute-start | bytes 393224 | tf_op jit(solution)/shard_map/ppermute | solution.py:308
  54.7 24.1 %collective-permute-start.6 = (bf16[8,64,128]{2,1,0:T(8,128)(2,1)S(1)}, bf16[8,64,128]{2,1,0:T(8,128)(2,1)S(1)}, u32[]{:S(2)}, u32[]{:S(2)}) collective-permute-start(bf16[8,64,128]{2,1,0:T(8,128)(2,1)S(1)} %get-tuple-element.27), channel_id=1, source_target_pairs={{2,4},{3,5},{4,2},{5,3},{10,12},{11,13},{12,10},{13,11},{18,20},{1... | collective-permute-start | bytes 393224 | tf_op jit(solution)/shard_map/ppermute | solution.py:308
  58.0 23.8 %collective-permute-start.7 = (bf16[8,64,128]{2,1,0:T(8,128)(2,1)S(1)}, bf16[8,64,128]{2,1,0:T(8,128)(2,1)S(1)}, u32[]{:S(2)}, u32[]{:S(2)}) collective-permute-start(bf16[8,64,128]{2,1,0:T(8,128)(2,1)S(1)} %get-tuple-element.28), channel_id=1, source_target_pairs={{2,5},{3,4},{4,3},{5,2},{10,13},{11,12},{12,11},{13,10},{18,21},{1... | collective-permute-start | bytes 393224 | tf_op jit(solution)/shard_map/ppermute | solution.py:308
  59.9 39.7 %collective-permute-start = (bf16[8,64,128]{2,1,0:T(8,128)(2,1)S(1)}, bf16[8,64,128]{2,1,0:T(8,128)(2,1)S(1)}, u32[]{:S(2)}, u32[]{:S(2)}) collective-permute-start(bf16[8,64,128]{2,1,0:T(8,128)(2,1)S(1)} %get-tuple-element.17), channel_id=1, source_target_pairs={{2,4},{3,5},{4,2},{5,3},{10,12},{11,13},{12,10},{13,11},{18,20},{1... | collective-permute-start | bytes 393224 | tf_op jit(solution)/shard_map/ppermute | solution.py:308
  63.0 36.6 %collective-permute-start.1 = (bf16[8,64,128]{2,1,0:T(8,128)(2,1)S(1)}, bf16[8,64,128]{2,1,0:T(8,128)(2,1)S(1)}, u32[]{:S(2)}, u32[]{:S(2)}) collective-permute-start(bf16[8,64,128]{2,1,0:T(8,128)(2,1)S(1)} %get-tuple-element.18), channel_id=1, source_target_pairs={{2,5},{3,4},{4,3},{5,2},{10,13},{11,12},{12,11},{13,10},{18,21},{1... | collective-permute-start | bytes 393224 | tf_op jit(solution)/shard_map/ppermute | solution.py:308
  76.0 21.6 %collective-permute-start.2 = (bf16[8,64,128]{2,1,0:T(8,128)(2,1)S(1)}, bf16[8,64,128]{2,1,0:T(8,128)(2,1)S(1)}, u32[]{:S(2)}, u32[]{:S(2)}) collective-permute-start(bf16[8,64,128]{2,1,0:T(8,128)(2,1)S(1)} %get-tuple-element.23), channel_id=1, source_target_pairs={{2,4},{3,5},{4,2},{5,3},{10,12},{11,13},{12,10},{13,11},{18,20},{1... | collective-permute-start | bytes 393224 | tf_op jit(solution)/shard_map/ppermute | solution.py:308
  78.7 18.8 %collective-permute-start.3 = (bf16[8,64,128]{2,1,0:T(8,128)(2,1)S(1)}, bf16[8,64,128]{2,1,0:T(8,128)(2,1)S(1)}, u32[]{:S(2)}, u32[]{:S(2)}) collective-permute-start(bf16[8,64,128]{2,1,0:T(8,128)(2,1)S(1)} %get-tuple-element.24), channel_id=1, source_target_pairs={{2,5},{3,4},{4,3},{5,2},{10,13},{11,12},{12,11},{13,10},{18,21},{1... | collective-permute-start | bytes 393224 | tf_op jit(solution)/shard_map/ppermute | solution.py:308
  81.8 13.8 %collective-permute-start.5 = (bf16[8,64,128]{2,1,0:T(8,128)(2,1)S(1)}, bf16[8,64,128]{2,1,0:T(8,128)(2,1)S(1)}, u32[]{:S(2)}, u32[]{:S(2)}) collective-permute-start(bf16[8,64,128]{2,1,0:T(8,128)(2,1)S(1)} %get-tuple-element.26), channel_id=1, source_target_pairs={{2,5},{3,4},{4,3},{5,2},{10,13},{11,12},{12,11},{13,10},{18,21},{1... | collective-permute-start | bytes 393224 | tf_op jit(solution)/shard_map/ppermute | solution.py:308

commit v11 on v10

--- a/solution.py
+++ b/solution.py
@@ -13,6 +13,9 @@
 ROWS = N // DEV
 COLS = N * N // DEV
 CHUNKS = COLS // 128
+EARLY = ((0, 1), (1, 1), (2, 2), (4, 4))
+LATER = ((0, 4), (4, 4))
+WHOLE = ((0, 8),)
 BF16 = jnp.bfloat16
 F32 = jnp.float32
 
@@ -63,15 +66,25 @@
 
     pl.semaphore_wait(barrier, DEV - 1)
 
-    def block(p, dest):
+    def group(rows, dest, src):
+        part = pl.ds(*rows)
         return pltpu.make_async_remote_copy(
-            src_ref=send.at[dest, p],
-            dst_ref=recv.at[me, p],
-            send_sem=send_sem.at[dest, p],
-            recv_sem=recv_sem.at[me, p],
+            src_ref=send.at[dest, part],
+            dst_ref=recv.at[src, part],
+            send_sem=send_sem.at[dest, rows[0]],
+            recv_sem=recv_sem.at[src, rows[0]],
             device_id={"dev": dest},
             device_id_type=pl.DeviceIdType.MESH,
         )
+
+    def start(rows, to):
+        for k in range(2):
+            group(rows, 2 * to + k, me).start()
+
+    def sent(groups, to):
+        for rows in groups:
+            for k in range(2):
+                group(rows, 2 * to + k, me).wait_send()
 
     low = iota((32, 8, 128), 2) < N
 
@@ -120,45 +133,42 @@
     for later in range(1, ROWS):
         load_row(later).start()
     chip_piece(jnp.where(is_edge, near, far))
-    for k in range(2):
-        block(0, 2 * jnp.where(is_edge, near, far) + k).start()
+    start(EARLY[0], jnp.where(is_edge, near, far))
     chip_piece(jnp.where(is_edge, far, outward))
 
     @pl.when(jnp.logical_not(is_edge))
     def _():
-        for k in range(2):
-            block(0, 2 * outward + k).start()
+        start(EARLY[0], outward)
 
     chip_piece(jnp.where(is_edge, last, near))
     chip_piece(chip)
-    block(0, partner).start()
+    group(EARLY[0], partner, me).start()
 
     def make_row(p, carry):
         load_row(p).wait()
         for h in range(2):
             half_row(p, h)
-        for k in range(2):
-            block(p, 2 * beside + k).start()
-
-        @pl.when(jnp.logical_not(is_edge))
-        def _():
-            for k in range(2):
-                block(p, 2 * far + k).start()
-
-        block(p, partner).start()
+        for rows in EARLY[1:]:
+            @pl.when(p == sum(rows) - 1)
+            def _():
+                start(rows, beside)
+
+                @pl.when(jnp.logical_not(is_edge))
+                def _():
+                    start(rows, far)
+
+                group(rows, partner, me).start()
+
         return carry
 
     lax.fori_loop(1, ROWS, make_row, 0)
 
     @pl.when(is_edge)
     def _():
-        for other in (far, last):
-            def far_row(p, carry):
-                for k in range(2):
-                    block(p, 2 * other + k).start()
-                return carry
-
-            lax.fori_loop(0, ROWS, far_row, 0)
+        for rows in LATER:
+            start(rows, far)
+        for rows in WHOLE:
+            start(rows, last)
 
     for side, dest in ((0, 2 * near + core), (1, 2 * near + 1 - core)):
         for chunk in range(CHUNKS):
@@ -186,53 +196,44 @@
 
     lax.fori_loop(0, ROWS // 2, own, 0)
 
-    def arrived(src, p):
-        pltpu.make_async_remote_copy(
-            src_ref=send.at[src, p],
-            dst_ref=recv.at[src, p],
-            send_sem=send_sem.at[src, p],
-            recv_sem=recv_sem.at[src, p],
-            device_id={"dev": src},
-            device_id_type=pl.DeviceIdType.MESH,
-        ).wait_recv()
-
-    def take(sources):
-        def body(t, carry):
+    def take(groups, sources):
+        for rows in groups:
             for src in sources:
-                arrived(src, 2 * t)
-                arrived(src, 2 * t + 1)
-                third(src, 2 * t, recv[src, 2 * t], recv[src, 2 * t + 1])
-            return carry
-
-        lax.fori_loop(0, ROWS // 2, body, 0)
-
-    take([partner])
+                group(rows, src, src).wait_recv()
+            if sum(rows) % 2 == 0:
+                begin = rows[0] // 2 * 2
+
+                def body(t, carry):
+                    for src in sources:
+                        p = begin + 2 * t
+                        third(src, p, recv[src, p], recv[src, p + 1])
+                    return carry
+
+                lax.fori_loop(0, (sum(rows) - begin) // 2, body, 0)
+
+    take(EARLY, [partner])
 
     @pl.when(jnp.logical_not(is_edge))
     def _():
         g_ref[:, pl.ds(pl.multiple_of(2 * N * near, 16), 2 * N), :] = jnp.zeros((8, 2 * N, COLS), BF16)
 
-    take([2 * beside, 2 * beside + 1])
-    take([2 * far, 2 * far + 1])
+    take(EARLY, [2 * beside, 2 * beside + 1])
+
+    for rows in EARLY:
+        group(rows, partner, me).wait_send()
+    sent(EARLY, beside)
 
     @pl.when(is_edge)
     def _():
-        take([2 * last, 2 * last + 1])
-
-    def sent_row(p, carry):
-        block(p, partner).wait_send()
-        for other in (beside, far):
-            for k in range(2):
-                block(p, 2 * other + k).wait_send()
-
-        @pl.when(is_edge)
-        def _():
-            for k in range(2):
-                block(p, 2 * last + k).wait_send()
-
-        return carry
-
-    lax.fori_loop(0, ROWS, sent_row, 0)
+        take(EARLY, [2 * far, 2 * far + 1])
+        take(WHOLE, [2 * last, 2 * last + 1])
+        sent(LATER, far)
+        sent(WHOLE, last)
+
+    @pl.when(jnp.logical_not(is_edge))
+    def _():
+        take(LATER, [2 * far, 2 * far + 1])
+        sent(EARLY, far)
 
 
 def most_kernel(g_ref, l4_ref, v_ref):
@@ -245,24 +246,18 @@
     core = lax.axis_index("dev") % 2
     for side, ref in ((core, same_ref), (1 - core, other_ref)):
         for p in range(0, ROWS, 2):
-            both = jnp.concatenate([ref[p], ref[p + 1]], axis=1)
-            g = jnp.dot(ct_ref[...], both, preferred_element_type=F32)
-            g0 = g[:, :128].reshape(8, 8, 128)
-            g1 = g[:, 128:].reshape(8, 8, 128)
-            g = jnp.concatenate([g0, g1], axis=1).astype(BF16)
+            g0 = jnp.dot(ct_ref[...], ref[p], preferred_element_type=F32).reshape(8, 8, 128)
+            g1 = jnp.dot(ct_ref[...], ref[p + 1], preferred_element_type=F32).reshape(8, 8, 128)
             at = pl.multiple_of(N * side + 8 * p, 16)
-            for ag in range(8):
-                g_vm[pl.ds(at, 16), 128 * ag:128 * ag + 128] = g[ag]
+            g_vm[:, pl.ds(at, 16), :] = jnp.concatenate([g0, g1], axis=1).astype(BF16)
 
     def put(ag):
         return pltpu.make_async_copy(v_vm.at[ag], v_hbm.at[:, pl.ds(8 * ag, 8), pl.ds(128 * chunk, 128)], v_sem.at[ag])
 
-    for pair in range(4):
-        part = jnp.dot(l4n_ref[...], g_vm[:, 256 * pair:256 * pair + 256], preferred_element_type=F32)
-        for k in range(2):
-            ag = 2 * pair + k
-            v_vm[ag] = (part[:, 128 * k:128 * k + 128] + most_ref[ag, :, 128 * chunk:128 * chunk + 128]).reshape(N, 8, 128)
-            put(ag).start()
+    for ag in range(8):
+        part = jnp.dot(l4n_ref[...], g_vm[ag], preferred_element_type=F32)
+        v_vm[ag] = (part + most_ref[ag, :, 128 * chunk:128 * chunk + 128]).reshape(N, 8, 128)
+        put(ag).start()
     for ag in range(8):
         put(ag).wait()
 
@@ -325,7 +320,7 @@
                 in_specs=[vmem] * 5 + ([] if v is None else [anywhere]),
                 out_specs=anywhere,
                 scratch_shapes=[
-                    pltpu.VMEM((2 * N, 8 * 128), BF16),
+                    pltpu.VMEM((8, 2 * N, 128), BF16),
                     pltpu.VMEM((8, N, 8, 128), F32),
                     pltpu.SemaphoreType.DMA((8,)),
                 ],

time: 102 us -> 101 us (level)
  the two profiles are of different devices: /device:TPU:21 before, /device:TPU:19 now
where the time goes in v11:
time: 101 us
  Pallas kernels  62.2 us (62%)
  starting transfers between devices  20.5 us (20%)
  waiting for transfers between devices  18.3 us (18%)
    pallas_call x1, Pallas kernels, local_transform(): pl.pallas_call(exchange_kernel, out_shape=outs, in_specs=[anywhere, anywh...  52.5 us
    ppermute x8, starting transfers between devices, local_transform(): pair.append(lax.ppermute(near[side * CHUNKS + chunk], 'dev', perm))  20.5 us
    ppermute x8, waiting for transfers between devices, local_transform(): pair.append(lax.ppermute(near[side * CHUNKS + chunk], 'dev', perm))  18.3 us
    pallas_call x4, Pallas kernels, local_transform(): pl.pallas_call(functools.partial(chunk_kernel, chunk), out_shape=sds((N,...  7.34 us
    pallas_call x1, Pallas kernels, local_transform(): pl.pallas_call(most_kernel, out_shape=sds((8, 8 * N, COLS), F32), in_spec...  2.34 us
  transfers between devices with their start and end apart: 8, of which 3 were waited for; matrix products, arithmetic and copies ran while one was open for 0% of the time, Pallas kernels for 8%

profile of v11, /device:TPU:19, one launch (start us, length us, event | category | flops | bytes accessed | tf_op | source)
XLA Modules:
  0.0 101.1 jit_solution(1270001000848649279)
XLA Ops:
  0.0 52.5 %exchange.1 = (bf16[8,512,512]{2,1,0:T(8,128)(2,1)S(1)}, bf16[512,512]{1,0:T(8,128)(2,1)S(1)}, bf16[512,128]{1,0:T(8,128)(2,1)S(1)}, bf16[64,64]{1,0:T(8,128)(2,...) custom-call(bf16[8,64,64,64]{3,2,1,0:T(8,128)(2,1)} %a_hbm.1, ...), custom_call_target="tpu_custom_call" | custom-call | tf_op jit(solution)/shard_map/exchange/pallas_call | solution.py:276
  52.5 1.9 %collective-permute-start.4 = (bf16[8,64,128]{2,1,0:T(8,128)(2,1)S(1)}, bf16[8,64,128]{2,1,0:T(8,128)(2,1)S(1)}, u32[]{:S(2)}, u32[]{:S(2)}) collective-permute-start(bf16[8,64,128]{2,1,0:T(8,128)(2,1)S(1)} %get-tuple-element.25), channel_id=1, source_target_pairs={{2,4},{3,5},{4,2},{5,3},{10,12},{11,13},{12,10},{13,11},{18,20},{1... | collective-permute-start | bytes 393224 | tf_op jit(solution)/shard_map/ppermute | solution.py:303
  54.4 3.4 %collective-permute-start.6 = (bf16[8,64,128]{2,1,0:T(8,128)(2,1)S(1)}, bf16[8,64,128]{2,1,0:T(8,128)(2,1)S(1)}, u32[]{:S(2)}, u32[]{:S(2)}) collective-permute-start(bf16[8,64,128]{2,1,0:T(8,128)(2,1)S(1)} %get-tuple-element.27), channel_id=1, source_target_pairs={{2,4},{3,5},{4,2},{5,3},{10,12},{11,13},{12,10},{13,11},{18,20},{1... | collective-permute-start | bytes 393224 | tf_op jit(solution)/shard_map/ppermute | solution.py:303
  57.8 1.9 %collective-permute-start.7 = (bf16[8,64,128]{2,1,0:T(8,128)(2,1)S(1)}, bf16[8,64,128]{2,1,0:T(8,128)(2,1)S(1)}, u32[]{:S(2)}, u32[]{:S(2)}) collective-permute-start(bf16[8,64,128]{2,1,0:T(8,128)(2,1)S(1)} %get-tuple-element.28), channel_id=1, source_target_pairs={{2,5},{3,4},{4,3},{5,2},{10,13},{11,12},{12,11},{13,10},{18,21},{1... | collective-permute-start | bytes 393224 | tf_op jit(solution)/shard_map/ppermute | solution.py:303
  59.7 2.3 %collective-permute-start = (bf16[8,64,128]{2,1,0:T(8,128)(2,1)S(1)}, bf16[8,64,128]{2,1,0:T(8,128)(2,1)S(1)}, u32[]{:S(2)}, u32[]{:S(2)}) collective-permute-start(bf16[8,64,128]{2,1,0:T(8,128)(2,1)S(1)} %get-tuple-element.17), channel_id=1, source_target_pairs={{2,4},{3,5},{4,2},{5,3},{10,12},{11,13},{12,10},{13,11},{18,20},{1... | collective-permute-start | bytes 393224 | tf_op jit(solution)/shard_map/ppermute | solution.py:303
  62.1 3.5 %collective-permute-start.1 = (bf16[8,64,128]{2,1,0:T(8,128)(2,1)S(1)}, bf16[8,64,128]{2,1,0:T(8,128)(2,1)S(1)}, u32[]{:S(2)}, u32[]{:S(2)}) collective-permute-start(bf16[8,64,128]{2,1,0:T(8,128)(2,1)S(1)} %get-tuple-element.18), channel_id=1, source_target_pairs={{2,5},{3,4},{4,3},{5,2},{10,13},{11,12},{12,11},{13,10},{18,21},{1... | collective-permute-start | bytes 393224 | tf_op jit(solution)/shard_map/ppermute | solution.py:303
  65.6 10.5 %collective-permute-done.4.same_ref = bf16[8,64,128]{2,1,0:T(8,128)(2,1)S(1)} collective-permute-done((bf16[8,64,128]{2,1,0:T(8,128)(2,1)S(1)}, bf16[8,64,128]{2,1,0:T(8,128)(2,1)S(1)}, u32[]{:S(2)}, u32[]{:S(2)}) %collective-permute-start.4) | collective-permute-done | bytes 131104 | tf_op jit(solution)/shard_map/ppermute | solution.py:303
  76.1 1.9 %collective-permute-start.2 = (bf16[8,64,128]{2,1,0:T(8,128)(2,1)S(1)}, bf16[8,64,128]{2,1,0:T(8,128)(2,1)S(1)}, u32[]{:S(2)}, u32[]{:S(2)}) collective-permute-start(bf16[8,64,128]{2,1,0:T(8,128)(2,1)S(1)} %get-tuple-element.23), channel_id=1, source_target_pairs={{2,4},{3,5},{4,2},{5,3},{10,12},{11,13},{12,10},{13,11},{18,20},{1... | collective-permute-start | bytes 393224 | tf_op jit(solution)/shard_map/ppermute | solution.py:303
  78.0 0.7 collective-permute-done.6.same_ref
  78.7 3.0 %collective-permute-start.3 = (bf16[8,64,128]{2,1,0:T(8,128)(2,1)S(1)}, bf16[8,64,128]{2,1,0:T(8,128)(2,1)S(1)}, u32[]{:S(2)}, u32[]{:S(2)}) collective-permute-start(bf16[8,64,128]{2,1,0:T(8,128)(2,1)S(1)} %get-tuple-element.24), channel_id=1, source_target_pairs={{2,5},{3,4},{4,3},{5,2},{10,13},{11,12},{12,11},{13,10},{18,21},{1... | collective-permute-start | bytes 393224 | tf_op jit(solution)/shard_map/ppermute | solution.py:303
  81.7 0.0 collective-permute-done.7.other_ref
  81.7 2.5 %collective-permute-start.5 = (bf16[8,64,128]{2,1,0:T(8,128)(2,1)S(1)}, bf16[8,64,128]{2,1,0:T(8,128)(2,1)S(1)}, u32[]{:S(2)}, u32[]{:S(2)}) collective-permute-start(bf16[8,64,128]{2,1,0:T(8,128)(2,1)S(1)} %get-tuple-element.26), channel_id=1, source_target_pairs={{2,5},{3,4},{4,3},{5,2},{10,13},{11,12},{12,11},{13,10},{18,21},{1... | collective-permute-start | bytes 393224 | tf_op jit(solution)/shard_map/ppermute | solution.py:303
  84.2 2.3 %most.1.most_ref = f32[8,512,512]{2,1,0:T(8,128)S(1)} custom-call(bf16[8,512,512]{2,1,0:T(8,128)(2,1)S(1)} %get-tuple-element.21.g_ref, bf16[512,512]{1,0:T(8,128)(2,1)S(1)} %get-tuple-element.22.l4_ref), custom_call_target="tpu_custom_call" | custom-call | flops 2147483648 | bytes 12582912 | tf_op jit(solution)/shard_map/most/pallas_call | solution.py:305
  86.6 1.8 %shard_map.28.refs_0_ = f32[64,64,512]{2,1,0:T(8,128)} custom-call(bf16[8,64,128]{2,1,0:T(8,128)(2,1)S(1)} %collective-permute-done.6.same_ref, bf16[8,64,128]{2,1,0:T(8,128)(2,1)S(1)} %collective-permute-done.7.other_ref, bf16[64,64]{1,0:T(8,128)(2,1)S(1)} %get-tuple-element.19.ct_ref, bf16[512,128]{1,0:T(8,128)(2,1)S(1)} %get-tuple-element.20.l4n_ref, ...), custom_call_target="tpu_custom_call" | custom-call | flops 134217728 | bytes 4194304 | tf_op jit(solution)/shard_map/pallas_call | solution.py:317
  88.4 7.1 %collective-permute-done.5.other_ref = bf16[8,64,128]{2,1,0:T(8,128)(2,1)S(1)} collective-permute-done((bf16[8,64,128]{2,1,0:T(8,128)(2,1)S(1)}, bf16[8,64,128]{2,1,0:T(8,128)(2,1)S(1)}, u32[]{:S(2)}, u32[]{:S(2)}) %collective-permute-start.5) | collective-permute-done | bytes 131104 | tf_op jit(solution)/shard_map/ppermute | solution.py:303
  95.5 1.8 %shard_map.29.refs_0_ = f32[64,64,512]{2,1,0:T(8,128)} custom-call(bf16[8,64,128]{2,1,0:T(8,128)(2,1)S(1)} %collective-permute-done.4.same_ref, bf16[8,64,128]{2,1,0:T(8,128)(2,1)S(1)} %collective-permute-done.5.other_ref, bf16[64,64]{1,0:T(8,128)(2,1)S(1)} %get-tuple-element.19.ct_ref, ...), custom_call_target="tpu_custom_call", output_to_operand_aliasing={{}: (5, {})} | custom-call | flops 134217728 | bytes 4194304 | tf_op jit(solution)/shard_map/pallas_call | solution.py:317
  97.4 0.0 collective-permute-done.2.same_ref
  97.4 0.0 collective-permute-done.3.other_ref
  97.4 1.8 %shard_map.30.refs_0_ = f32[64,64,512]{2,1,0:T(8,128)} custom-call(bf16[8,64,128]{2,1,0:T(8,128)(2,1)S(1)} %collective-permute-done.2.same_ref, bf16[8,64,128]{2,1,0:T(8,128)(2,1)S(1)} %collective-permute-done.3.other_ref, bf16[64,64]{1,0:T(8,128)(2,1)S(1)} %get-tuple-element.19.ct_ref, ...), custom_call_target="tpu_custom_call", output_to_operand_aliasing={{}: (5, {})} | custom-call | flops 134217728 | bytes 4194304 | tf_op jit(solution)/shard_map/pallas_call | solution.py:317
  99.2 0.0 collective-permute-done.same_ref
  99.2 0.0 collective-permute-done.1.other_ref
  99.3 1.8 %shard_map.31 = f32[64,64,512]{2,1,0:T(8,128)} custom-call(bf16[8,64,128]{2,1,0:T(8,128)(2,1)S(1)} %collective-permute-done.same_ref, bf16[8,64,128]{2,1,0:T(8,128)(2,1)S(1)} %collective-permute-done.1.other_ref, bf16[64,64]{1,0:T(8,128)(2,1)S(1)} %get-tuple-element.19.ct_ref, ...), custom_call_target="tpu_custom_call", output_to_operand_aliasing={{}: (5, {})} | custom-call | flops 134217728 | bytes 4194304 | tf_op jit(solution)/shard_map/pallas_call | solution.py:317
Async XLA Ops:
  52.5 23.6 %collective-permute-start.4 = (bf16[8,64,128]{2,1,0:T(8,128)(2,1)S(1)}, bf16[8,64,128]{2,1,0:T(8,128)(2,1)S(1)}, u32[]{:S(2)}, u32[]{:S(2)}) collective-permute-start(bf16[8,64,128]{2,1,0:T(8,128)(2,1)S(1)} %get-tuple-element.25), channel_id=1, source_target_pairs={{2,4},{3,5},{4,2},{5,3},{10,12},{11,13},{12,10},{13,11},{18,20},{1... | collective-permute-start | bytes 393224 | tf_op jit(solution)/shard_map/ppermute | solution.py:303
  54.4 24.2 %collective-permute-start.6 = (bf16[8,64,128]{2,1,0:T(8,128)(2,1)S(1)}, bf16[8,64,128]{2,1,0:T(8,128)(2,1)S(1)}, u32[]{:S(2)}, u32[]{:S(2)}) collective-permute-start(bf16[8,64,128]{2,1,0:T(8,128)(2,1)S(1)} %get-tuple-element.27), channel_id=1, source_target_pairs={{2,4},{3,5},{4,2},{5,3},{10,12},{11,13},{12,10},{13,11},{18,20},{1... | collective-permute-start | bytes 393224 | tf_op jit(solution)/shard_map/ppermute | solution.py:303
  57.8 23.9 %collective-permute-start.7 = (bf16[8,64,128]{2,1,0:T(8,128)(2,1)S(1)}, bf16[8,64,128]{2,1,0:T(8,128)(2,1)S(1)}, u32[]{:S(2)}, u32[]{:S(2)}) collective-permute-start(bf16[8,64,128]{2,1,0:T(8,128)(2,1)S(1)} %get-tuple-element.28), channel_id=1, source_target_pairs={{2,5},{3,4},{4,3},{5,2},{10,13},{11,12},{12,11},{13,10},{18,21},{1... | collective-permute-start | bytes 393224 | tf_op jit(solution)/shard_map/ppermute | solution.py:303
  59.7 39.5 %collective-permute-start = (bf16[8,64,128]{2,1,0:T(8,128)(2,1)S(1)}, bf16[8,64,128]{2,1,0:T(8,128)(2,1)S(1)}, u32[]{:S(2)}, u32[]{:S(2)}) collective-permute-start(bf16[8,64,128]{2,1,0:T(8,128)(2,1)S(1)} %get-tuple-element.17), channel_id=1, source_target_pairs={{2,4},{3,5},{4,2},{5,3},{10,12},{11,13},{12,10},{13,11},{18,20},{1... | collective-permute-start | bytes 393224 | tf_op jit(solution)/shard_map/ppermute | solution.py:303
  62.1 37.2 %collective-permute-start.1 = (bf16[8,64,128]{2,1,0:T(8,128)(2,1)S(1)}, bf16[8,64,128]{2,1,0:T(8,128)(2,1)S(1)}, u32[]{:S(2)}, u32[]{:S(2)}) collective-permute-start(bf16[8,64,128]{2,1,0:T(8,128)(2,1)S(1)} %get-tuple-element.18), channel_id=1, source_target_pairs={{2,5},{3,4},{4,3},{5,2},{10,13},{11,12},{12,11},{13,10},{18,21},{1... | collective-permute-start | bytes 393224 | tf_op jit(solution)/shard_map/ppermute | solution.py:303
  76.1 21.3 %collective-permute-start.2 = (bf16[8,64,128]{2,1,0:T(8,128)(2,1)S(1)}, bf16[8,64,128]{2,1,0:T(8,128)(2,1)S(1)}, u32[]{:S(2)}, u32[]{:S(2)}) collective-permute-start(bf16[8,64,128]{2,1,0:T(8,128)(2,1)S(1)} %get-tuple-element.23), channel_id=1, source_target_pairs={{2,4},{3,5},{4,2},{5,3},{10,12},{11,13},{12,10},{13,11},{18,20},{1... | collective-permute-start | bytes 393224 | tf_op jit(solution)/shard_map/ppermute | solution.py:303
  78.7 18.7 %collective-permute-start.3 = (bf16[8,64,128]{2,1,0:T(8,128)(2,1)S(1)}, bf16[8,64,128]{2,1,0:T(8,128)(2,1)S(1)}, u32[]{:S(2)}, u32[]{:S(2)}) collective-permute-start(bf16[8,64,128]{2,1,0:T(8,128)(2,1)S(1)} %get-tuple-element.24), channel_id=1, source_target_pairs={{2,5},{3,4},{4,3},{5,2},{10,13},{11,12},{12,11},{13,10},{18,21},{1... | collective-permute-start | bytes 393224 | tf_op jit(solution)/shard_map/ppermute | solution.py:303
  81.7 13.8 %collective-permute-start.5 = (bf16[8,64,128]{2,1,0:T(8,128)(2,1)S(1)}, bf16[8,64,128]{2,1,0:T(8,128)(2,1)S(1)}, u32[]{:S(2)}, u32[]{:S(2)}) collective-permute-start(bf16[8,64,128]{2,1,0:T(8,128)(2,1)S(1)} %get-tuple-element.26), channel_id=1, source_target_pairs={{2,5},{3,4},{4,3},{5,2},{10,13},{11,12},{12,11},{13,10},{18,21},{1... | collective-permute-start | bytes 393224 | tf_op jit(solution)/shard_map/ppermute | solution.py:303
